TPU v7x, 32 devices: a whole 2x2x4 slice. The times are simulated.
32 devices in a mesh: gx: 4 (over x, core), gy: 2 (over y), gz: 4 (over z).
Axes of the slice: x: 2, y: 2, z: 4, core: 2. Of those that a mesh axis runs over, the one named last changes fastest.
Arguments:
- fields: float32 [32, 32, 16, 512], P(None, 'gx', 'gy', 'gz'), may hold values from -8 to 8
- strength: float32 [32], replicated, may hold values from 0.3 to 1
Outputs:
- filtered: float32 [32, 32, 16, 512], P(None, 'gx', 'gy', 'gz')
All inputs are finite; a program needn't handle non-finite values.
Results may differ from a plain program's by a relative error of at most 0.00002.
Values sent between devices are 32-bit elements; how exact they have to be, the bound alone decides.
A program may use at most 64 MiB of HBM per device.

v0:
```python
import functools
import jax
import jax.numpy as jnp
from jax import lax
from jax.experimental import pallas as pl
from jax.experimental.pallas import tpu as pltpu
from jax.sharding import PartitionSpec as P

MESH = pl.DeviceIdType.MESH
REACH = 5
SLOT = 8
WEIGHTS = [-252.0, 210.0, -120.0, 45.0, -10.0, 1.0]
CUTS = (4, 4, 4, 4, 4, 4, 4, 2, 2)


def weight_of(offset):
    return WEIGHTS[abs(offset)] if abs(offset) <= REACH else 0.0


def row_weights(rows, lanes, roll, bases):
    row = lax.broadcasted_iota(jnp.int32, (rows, lanes), 0)
    out = jnp.zeros((rows, lanes), jnp.float32)
    for i in range(rows):
        value = sum(weight_of((i + roll) % rows + base - i) for base in bases)
        if value:
            out = jnp.where(row == i, value, out)
    return out


def rolled_rows(block, roll):
    rows = block.shape[1]
    return block if roll == 0 else pltpu.roll(block, rows - roll, 1)


def rows_sum(block, weights):
    total = None
    for roll, weight in enumerate(weights):
        term = weight[None] * rolled_rows(block, roll)
        total = term if total is None else total + term
    return total


def kernel(nx, ny, nz, cuts, fields, strength_in, out, strength, u, acc, xl, xr, ys, packed, landed,
           in_sem, x_send, x_recv, y_send, y_recv, z_send, z_recv, answers):
    species, cx, cy, cz = u.shape
    groups = cz // SLOT
    rows_packed = packed.shape[1]
    px, py, pz = lax.axis_index("gx"), lax.axis_index("gy"), lax.axis_index("gz")
    x_left, x_right = lax.rem(px + nx - 1, nx), lax.rem(px + 1, nx)
    y_left, y_right = lax.rem(py + ny - 1, ny), lax.rem(py + 1, ny)
    z_left, z_right = lax.rem(pz + nz - 1, nz), lax.rem(pz + 1, nz)
    y_peers = [y_right] if ny == 2 else [y_right, y_left]

    barrier = pltpu.get_barrier_semaphore()
    to_left, to_right = (px, py, z_left), (px, py, z_right)
    left_x, right_x = (x_left, py, pz), (x_right, py, pz)
    first_x, last_x, first_z, last_z = px == 0, px == nx - 1, pz == 0, pz == nz - 1

    def tell(semaphore, peer):
        pl.semaphore_signal(semaphore, inc=1, device_id=peer, device_id_type=MESH)

    for peer in y_peers:
        tell(barrier, (px, peer, pz))
    pl.when(px < nx - 1)(lambda: tell(barrier, right_x))
    pl.when(first_x)(lambda: tell(barrier, left_x))
    pl.when(pz < nz - 1)(lambda: tell(barrier, to_right))

    spans = []
    begin = 0
    for size in cuts:
        spans.append((begin, size))
        begin += size
    loads = []
    for k, (begin, size) in enumerate(spans):
        part = pl.ds(begin, size)
        loads.append(pltpu.make_async_copy(fields.at[part], u.at[part], in_sem.at[k]))
    greeters = sum(c.astype(jnp.int32) for c in (px > 0, last_x, pz > 0))
    pl.semaphore_wait(barrier, len(y_peers) + greeters)

    y_copies, x_copies = [], []
    for k, (begin, size) in enumerate(spans):
        part = pl.ds(begin, size)
        row = []
        for side, peer in enumerate(y_peers):
            row.append(pltpu.make_async_remote_copy(
                src_ref=fields.at[part], dst_ref=ys.at[side, part],
                send_sem=y_send.at[side, k], recv_sem=y_recv.at[side, k],
                device_id=(px, peer, pz), device_id_type=MESH))
        y_copies.append(row)
        x_copies.append([
            pltpu.make_async_remote_copy(
                src_ref=u.at[part, pl.ds(cx - REACH, REACH)], dst_ref=xl.at[part],
                send_sem=x_send.at[0, k], recv_sem=x_recv.at[0, k],
                device_id=(x_right, py, pz), device_id_type=MESH),
            pltpu.make_async_remote_copy(
                src_ref=u.at[part, pl.ds(0, REACH)], dst_ref=xr.at[part],
                send_sem=x_send.at[1, k], recv_sem=x_recv.at[1, k],
                device_id=(x_left, py, pz), device_id_type=MESH),
        ])
    for row in y_copies:
        for copy in row:
            copy.start()
    gains = pltpu.make_async_copy(strength_in, strength, in_sem.at[len(cuts)])
    gains.start()
    for load in loads:
        load.start()
    pl.when(px > 0)(lambda: tell(answers.at[0], left_x))
    pl.when(last_x)(lambda: tell(answers.at[1], right_x))
    pl.when(last_z)(lambda: tell(answers.at[2], to_left))
    gains.wait()
    for load in loads:
        load.wait()
    pl.when(px < nx - 1)(lambda: pl.semaphore_wait(answers.at[0], 1))
    pl.when(first_x)(lambda: pl.semaphore_wait(answers.at[1], 1))
    for row in x_copies:
        for copy in row:
            copy.start()

    lane = lax.broadcasted_iota(jnp.int32, (cx, cy, cz), 2)
    slot = lane // SLOT
    for p in range(rows_packed):
        first = p * groups
        here = min(groups, species - first)

        def pack(g, carry):
            head, tail = carry
            v = u[first + g]
            mine = slot == g
            head = jnp.where(mine, pltpu.roll(v, g * SLOT, 2), head)
            tail = jnp.where(mine, pltpu.roll(v, lax.rem((g + 1) * SLOT, cz), 2), tail)
            return head, tail

        zero = jnp.zeros((cx, cy, cz), jnp.float32)
        head, tail = lax.fori_loop(0, here, pack, (zero, zero))
        packed[0, p] = head
        packed[1, p] = tail

    pl.when(pz < nz - 1)(lambda: pl.semaphore_wait(answers.at[2], 1))
    pl.when(jnp.logical_and(pz > 0, pz < nz - 1))(lambda: tell(answers.at[2], to_left))
    pl.when(first_z)(lambda: tell(answers.at[3], to_left))
    pl.when(last_z)(lambda: pl.semaphore_wait(answers.at[3], 1))
    z_copies = [
        pltpu.make_async_remote_copy(
            src_ref=packed.at[side], dst_ref=landed.at[side],
            send_sem=z_send.at[side], recv_sem=z_recv.at[side],
            device_id=(px, py, peer), device_id_type=MESH)
        for side, peer in enumerate((z_left, z_right))
    ]
    for copy in z_copies:
        copy.start()

    own = [row_weights(cy, cz, r, (0,)) for r in range(cy)]
    if ny == 2:
        remote = [[row_weights(cy, cz, r, (cy, -cy)) for r in range(cy)]]
    else:
        remote = [[row_weights(cy, cz, r, (base,)) for r in range(cy)] for base in (-cy, cy)]

    for copy in z_copies:
        copy.wait()

    def along_z(s, _):
        v = u[s]
        p, g = s // groups, lax.rem(s, groups)
        after = pltpu.roll(landed[0, p], lax.rem(cz - g * SLOT, cz), 2)
        before = pltpu.roll(landed[1, p], cz - (g + 1) * SLOT, 2)
        total = (2.0 * WEIGHTS[0]) * v
        for d in range(1, REACH + 1):
            up = pltpu.roll(jnp.where(lane < d, after, v), cz - d, 2)
            down = pltpu.roll(jnp.where(lane >= cz - d, before, v), d, 2)
            total = total + WEIGHTS[d] * (up + down)
        acc[s] = total + rows_sum(v, own)
        return 0

    lax.fori_loop(0, species, along_z, 0)

    def along_x(s, _):
        cells = [xl[s, i] for i in range(REACH)] + [u[s, i] for i in range(cx)]
        cells += [xr[s, i] for i in range(REACH)]
        for i in range(cx):
            total = acc[s, i]
            for d in range(1, REACH + 1):
                total = total + WEIGHTS[d] * (cells[REACH + i - d] + cells[REACH + i + d])
            acc[s, i] = total
        return 0

    def along_y(s, _):
        total = acc[s]
        for side, weights in enumerate(remote):
            total = total + rows_sum(ys[side, s], weights)
        out[s] = u[s] + (strength[s] * (1.0 / 1024.0)) * total
        return 0

    for k, (begin, size) in enumerate(spans):
        part = pl.ds(begin, size)
        for copy in x_copies[k]:
            copy.wait_recv()
        lax.fori_loop(begin, begin + size, along_x, 0)
        for copy in y_copies[k]:
            copy.wait_recv()
        lax.fori_loop(begin, begin + size, along_y, 0)
    for k in range(len(spans)):
        for copy in y_copies[k] + x_copies[k]:
            copy.wait_send()


def local(nx, ny, nz, fields, strength):
    species, cx, cy, cz = fields.shape
    cuts = CUTS if sum(CUTS) == species else (1,) * species
    pieces = len(cuts)
    sides = 1 if ny == 2 else 2
    groups = cz // SLOT
    rows_packed = -(-species // groups)
    block = (species, cx, cy, cz)
    dma = pltpu.SemaphoreType.DMA
    return pl.pallas_call(
        functools.partial(kernel, nx, ny, nz, cuts),
        out_shape=pltpu.VMEM(block, jnp.float32),
        in_specs=[pl.BlockSpec(memory_space=pltpu.HBM), pl.BlockSpec(memory_space=pl.ANY)],
        out_specs=pl.BlockSpec(memory_space=pltpu.VMEM),
        scratch_shapes=[
            pltpu.SMEM((species,), jnp.float32),
            pltpu.VMEM(block, jnp.float32),
            pltpu.VMEM(block, jnp.float32),
            pltpu.VMEM((species, REACH, cy, cz), jnp.float32),
            pltpu.VMEM((species, REACH, cy, cz), jnp.float32),
            pltpu.VMEM((sides,) + block, jnp.float32),
            pltpu.VMEM((2, rows_packed, cx, cy, cz), jnp.float32),
            pltpu.VMEM((2, rows_packed, cx, cy, cz), jnp.float32),
            dma((pieces + 1,)),
            dma((2, pieces)),
            dma((2, pieces)),
            dma((sides, pieces)),
            dma((sides, pieces)),
            dma((2,)),
            dma((2,)),
            pltpu.SemaphoreType.REGULAR((4,)),
        ],
        compiler_params=pltpu.CompilerParams(collective_id=0, has_side_effects=True, vmem_limit_bytes=56 * 1024 * 1024),
        name="filter_pass",
    )(fields, strength)


def solution(mesh):
    sizes = mesh.shape
    return jax.shard_map(
        functools.partial(local, sizes["gx"], sizes["gy"], sizes["gz"]),
        mesh=mesh,
        in_specs=(P(None, "gx", "gy", "gz"), P()),
        out_specs=P(None, "gx", "gy", "gz"),
        check_vma=False,
    )
```

profile of v0, /device:TPU:0, one launch (start us, length us, event | category | flops | bytes accessed | tf_op | source)
XLA Modules:
  0.0 28.8 jit_solution(16111967532924225706)
XLA Ops:
  0.0 27.8 %filter_pass.1 = f32[32,8,8,128]{3,2,1,0:T(8,128)S(1)} custom-call(f32[32,8,8,128]{3,2,1,0:T(8,128)} %fields.1, f32[32]{0:T(128)} %strength_in.1), custom_call_target="tpu_custom_call" | custom-call | tf_op jit(solution)/shard_map/filter_pass/pallas_call | solution.py:215
  27.8 1.0 %copy.4 = f32[32,8,8,128]{3,2,1,0:T(8,128)} copy(f32[32,8,8,128]{3,2,1,0:T(8,128)S(1)} %filter_pass.1) | data formatting | bytes 2097152
where the time goes:
time: 28.9 us; the launch traced here: 28.8 us
  Pallas kernels  27.8 us (96%)
  local copies, waits for them, and re-layouts  0.97 us (3%)
    pallas_call x1, Pallas kernels, local(): pl.pallas_call(functools.partial(kernel, nx, ny, nz, cuts), out_shape=plt...  27.8 us
    unnamed x1, local copies, waits for them, and re-layouts  0.97 us

commit v1 on v0

--- a/solution.py
+++ b/solution.py
@@ -10,7 +10,8 @@
 REACH = 5
 SLOT = 8
 WEIGHTS = [-252.0, 210.0, -120.0, 45.0, -10.0, 1.0]
-CUTS = (4, 4, 4, 4, 4, 4, 4, 2, 2)
+CUTS = (2, 8, 8, 6, 3, 2, 2, 1)
+EARLY = 4
 
 
 def weight_of(offset):
@@ -40,8 +41,8 @@
     return total
 
 
-def kernel(nx, ny, nz, cuts, fields, strength_in, out, strength, u, acc, xl, xr, ys, packed, landed,
-           in_sem, x_send, x_recv, y_send, y_recv, z_send, z_recv, answers):
+def kernel(nx, ny, nz, cuts, early, fields, strength_in, out, strength, u, acc, xl, xr, ys, packed, landed,
+           in_sem, x_send, x_recv, y_send, y_recv, z_send, z_recv, answers, turn):
     species, cx, cy, cz = u.shape
     groups = cz // SLOT
     rows_packed = packed.shape[1]
@@ -74,16 +75,20 @@
     for k, (begin, size) in enumerate(spans):
         part = pl.ds(begin, size)
         loads.append(pltpu.make_async_copy(fields.at[part], u.at[part], in_sem.at[k]))
-    greeters = sum(c.astype(jnp.int32) for c in (px > 0, last_x, pz > 0))
-    pl.semaphore_wait(barrier, len(y_peers) + greeters)
-
+    gains = pltpu.make_async_copy(strength_in, strength, in_sem.at[len(cuts)])
+    for load in loads:
+        load.start()
+    gains.start()
+
+    held = early < len(cuts)
+    odd = lax.rem(px, 2) == 1
     y_copies, x_copies = [], []
     for k, (begin, size) in enumerate(spans):
         part = pl.ds(begin, size)
         row = []
         for side, peer in enumerate(y_peers):
             row.append(pltpu.make_async_remote_copy(
-                src_ref=fields.at[part], dst_ref=ys.at[side, part],
+                src_ref=u.at[part], dst_ref=ys.at[side, part],
                 send_sem=y_send.at[side, k], recv_sem=y_recv.at[side, k],
                 device_id=(px, peer, pz), device_id_type=MESH))
         y_copies.append(row)
@@ -97,19 +102,30 @@
                 send_sem=x_send.at[1, k], recv_sem=x_recv.at[1, k],
                 device_id=(x_left, py, pz), device_id_type=MESH),
         ])
-    for row in y_copies:
-        for copy in row:
-            copy.start()
-    gains = pltpu.make_async_copy(strength_in, strength, in_sem.at[len(cuts)])
-    gains.start()
-    for load in loads:
-        load.start()
+
+    def start_y(rows):
+        for row in rows:
+            for copy in row:
+                copy.start()
+
+    def sent_y(rows):
+        for row in rows:
+            for copy in row:
+                copy.wait_send()
+
+    greeters = sum(c.astype(jnp.int32) for c in (px > 0, last_x, pz > 0))
+    pl.semaphore_wait(barrier, len(y_peers) + greeters)
+    for load, row in zip(loads[:early], y_copies[:early]):
+        load.wait()
+        start_y([row])
+    for load in loads[early:]:
+        load.wait()
+    if held:
+        pl.when(jnp.logical_not(odd))(lambda: start_y(y_copies[early:]))
     pl.when(px > 0)(lambda: tell(answers.at[0], left_x))
     pl.when(last_x)(lambda: tell(answers.at[1], right_x))
     pl.when(last_z)(lambda: tell(answers.at[2], to_left))
     gains.wait()
-    for load in loads:
-        load.wait()
     pl.when(px < nx - 1)(lambda: pl.semaphore_wait(answers.at[0], 1))
     pl.when(first_x)(lambda: pl.semaphore_wait(answers.at[1], 1))
     for row in x_copies:
@@ -190,30 +206,49 @@
         out[s] = u[s] + (strength[s] * (1.0 / 1024.0)) * total
         return 0
 
+    def take_turn():
+        def pass_on():
+            sent_y(y_copies[:early + 1])
+            tell(turn, right_x)
+
+        def go_on():
+            pl.semaphore_wait(turn, 1)
+            start_y(y_copies[early:])
+
+        pl.when(odd)(go_on)
+        pl.when(jnp.logical_not(odd))(pass_on)
+
     for k, (begin, size) in enumerate(spans):
-        part = pl.ds(begin, size)
+        if k == early:
+            take_turn()
         for copy in x_copies[k]:
             copy.wait_recv()
         lax.fori_loop(begin, begin + size, along_x, 0)
         for copy in y_copies[k]:
             copy.wait_recv()
         lax.fori_loop(begin, begin + size, along_y, 0)
-    for k in range(len(spans)):
-        for copy in y_copies[k] + x_copies[k]:
+    for row in x_copies:
+        for copy in row:
             copy.wait_send()
+    if held:
+        pl.when(odd)(lambda: sent_y(y_copies[:early + 1]))
+        sent_y(y_copies[early + 1:])
+    else:
+        sent_y(y_copies)
 
 
 def local(nx, ny, nz, fields, strength):
     species, cx, cy, cz = fields.shape
     cuts = CUTS if sum(CUTS) == species else (1,) * species
     pieces = len(cuts)
+    early = EARLY if sum(CUTS) == species and nx % 2 == 0 else pieces
     sides = 1 if ny == 2 else 2
     groups = cz // SLOT
     rows_packed = -(-species // groups)
     block = (species, cx, cy, cz)
     dma = pltpu.SemaphoreType.DMA
     return pl.pallas_call(
-        functools.partial(kernel, nx, ny, nz, cuts),
+        functools.partial(kernel, nx, ny, nz, cuts, early),
         out_shape=pltpu.VMEM(block, jnp.float32),
         in_specs=[pl.BlockSpec(memory_space=pltpu.HBM), pl.BlockSpec(memory_space=pl.ANY)],
         out_specs=pl.BlockSpec(memory_space=pltpu.VMEM),
@@ -234,6 +269,7 @@
             dma((2,)),
             dma((2,)),
             pltpu.SemaphoreType.REGULAR((4,)),
+            pltpu.SemaphoreType.REGULAR,
         ],
         compiler_params=pltpu.CompilerParams(collective_id=0, has_side_effects=True, vmem_limit_bytes=56 * 1024 * 1024),
         name="filter_pass",

time: 28.9 us -> 32.3 us (1.12)
  the two profiles are of different devices: /device:TPU:0 before, /device:TPU:1 now
where the time goes in v1:
time: 32.3 us; the launch traced here: 32.1 us
  Pallas kernels  31.1 us (96%)
  local copies, waits for them, and re-layouts  0.97 us (3%)
    pallas_call x1, Pallas kernels, local(): pl.pallas_call(functools.partial(kernel, nx, ny, nz, cuts, early), out_sh...  31.1 us
    unnamed x1, local copies, waits for them, and re-layouts  0.97 us

profile of v1, /device:TPU:1, one launch (start us, length us, event | category | flops | bytes accessed | tf_op | source)
XLA Modules:
  0.0 32.1 jit_solution(120939725359740762)
XLA Ops:
  0.0 31.1 %filter_pass.1 = f32[32,8,8,128]{3,2,1,0:T(8,128)S(1)} custom-call(f32[32,8,8,128]{3,2,1,0:T(8,128)} %fields.1, f32[32]{0:T(128)} %strength_in.1), custom_call_target="tpu_custom_call" | custom-call | tf_op jit(solution)/shard_map/filter_pass/pallas_call | solution.py:250
  31.1 1.0 %copy.4 = f32[32,8,8,128]{3,2,1,0:T(8,128)} copy(f32[32,8,8,128]{3,2,1,0:T(8,128)S(1)} %filter_pass.1) | data formatting | bytes 2097152

commit v2 on v1

--- a/solution.py
+++ b/solution.py
@@ -12,6 +12,19 @@
 WEIGHTS = [-252.0, 210.0, -120.0, 45.0, -10.0, 1.0]
 CUTS = (2, 8, 8, 6, 3, 2, 2, 1)
 EARLY = 4
+X_PIECES = 2
+AT_ONCE = (8, 4, 8)
+
+
+def each(begin, count, at_once, body, carry=0):
+    step = at_once if count % at_once == 0 else 1
+
+    def steps(k, carry):
+        for i in range(step):
+            carry = body(begin + k * step + i, carry)
+        return carry
+
+    return lax.fori_loop(0, count // step, steps, carry)
 
 
 def weight_of(offset):
@@ -28,6 +41,26 @@
     return out
 
 
+def lane_weights(lanes, bases, centre):
+    source = lax.broadcasted_iota(jnp.int32, (lanes, lanes), 0)
+    offset = source - lax.broadcasted_iota(jnp.int32, (lanes, lanes), 1)
+    out = jnp.zeros((lanes, lanes), jnp.float32)
+    for base in bases:
+        for d in range(-REACH, REACH + 1):
+            out = jnp.where(offset + base == d, centre if d == 0 else weight_of(d), out)
+    return out.astype(jnp.bfloat16)
+
+
+def along_lanes(rows, weights):
+    total = None
+    for part in range(3):
+        piece = rows.astype(jnp.bfloat16)
+        rows = rows - piece.astype(jnp.float32)
+        term = jnp.dot(piece, weights, preferred_element_type=jnp.float32)
+        total = term if total is None else total + term
+    return total
+
+
 def rolled_rows(block, roll):
     rows = block.shape[1]
     return block if roll == 0 else pltpu.roll(block, rows - roll, 1)
@@ -41,7 +74,7 @@
     return total
 
 
-def kernel(nx, ny, nz, cuts, early, fields, strength_in, out, strength, u, acc, xl, xr, ys, packed, landed,
+def kernel(nx, ny, nz, cuts, early, x_size, fields, strength_in, out, strength, u, acc, xl, xr, ys, packed, landed,
            in_sem, x_send, x_recv, y_send, y_recv, z_send, z_recv, answers, turn):
     species, cx, cy, cz = u.shape
     groups = cz // SLOT
@@ -92,6 +125,9 @@
                 send_sem=y_send.at[side, k], recv_sem=y_recv.at[side, k],
                 device_id=(px, peer, pz), device_id_type=MESH))
         y_copies.append(row)
+    x_spans = [(at, x_size) for at in range(0, species, x_size)]
+    for k, (begin, size) in enumerate(x_spans):
+        part = pl.ds(begin, size)
         x_copies.append([
             pltpu.make_async_remote_copy(
                 src_ref=u.at[part, pl.ds(cx - REACH, REACH)], dst_ref=xl.at[part],
@@ -124,7 +160,8 @@
         pl.when(jnp.logical_not(odd))(lambda: start_y(y_copies[early:]))
     pl.when(px > 0)(lambda: tell(answers.at[0], left_x))
     pl.when(last_x)(lambda: tell(answers.at[1], right_x))
-    pl.when(last_z)(lambda: tell(answers.at[2], to_left))
+    pl.when(pz > 0)(lambda: tell(answers.at[2], to_left))
+    pl.when(last_z)(lambda: tell(answers.at[4], to_left))
     gains.wait()
     pl.when(px < nx - 1)(lambda: pl.semaphore_wait(answers.at[0], 1))
     pl.when(first_x)(lambda: pl.semaphore_wait(answers.at[1], 1))
@@ -147,14 +184,10 @@
             return head, tail
 
         zero = jnp.zeros((cx, cy, cz), jnp.float32)
-        head, tail = lax.fori_loop(0, here, pack, (zero, zero))
+        head, tail = each(0, here, AT_ONCE[0], pack, (zero, zero))
         packed[0, p] = head
         packed[1, p] = tail
 
-    pl.when(pz < nz - 1)(lambda: pl.semaphore_wait(answers.at[2], 1))
-    pl.when(jnp.logical_and(pz > 0, pz < nz - 1))(lambda: tell(answers.at[2], to_left))
-    pl.when(first_z)(lambda: tell(answers.at[3], to_left))
-    pl.when(last_z)(lambda: pl.semaphore_wait(answers.at[3], 1))
     z_copies = [
         pltpu.make_async_remote_copy(
             src_ref=packed.at[side], dst_ref=landed.at[side],
@@ -162,32 +195,57 @@
             device_id=(px, py, peer), device_id_type=MESH)
         for side, peer in enumerate((z_left, z_right))
     ]
-    for copy in z_copies:
-        copy.start()
+
+    def start_right():
+        pl.semaphore_wait(answers.at[2], 1)
+        z_copies[1].start()
+
+    def pass_token():
+        pl.semaphore_wait(answers.at[4], 1)
+        tell(answers.at[4], to_left)
+
+    def close_ring():
+        pl.semaphore_wait(answers.at[4], 1)
+        tell(answers.at[3], to_left)
+        z_copies[0].start()
+
+    def end_ring():
+        pl.semaphore_wait(answers.at[3], 1)
+        z_copies[1].start()
+
+    pl.when(pz > 0)(z_copies[0].start)
+    pl.when(pz < nz - 1)(start_right)
+    pl.when(jnp.logical_and(pz > 0, pz < nz - 1))(pass_token)
+    pl.when(first_z)(close_ring)
 
     own = [row_weights(cy, cz, r, (0,)) for r in range(cy)]
     if ny == 2:
         remote = [[row_weights(cy, cz, r, (cy, -cy)) for r in range(cy)]]
     else:
         remote = [[row_weights(cy, cz, r, (base,)) for r in range(cy)] for base in (-cy, cy)]
-
+    inside = lane_weights(cz, (0,), 2.0 * WEIGHTS[0])
+    across = lane_weights(cz, (cz, -cz), WEIGHTS[0])
+
+    def along_own(s, _):
+        v = u[s]
+        total = along_lanes(v.reshape(cx * cy, cz), inside).reshape(cx, cy, cz)
+        acc[s] = total + rows_sum(v, own)
+        return 0
+
+    each(0, species, AT_ONCE[1], along_own)
+    pl.when(last_z)(end_ring)
     for copy in z_copies:
         copy.wait()
 
     def along_z(s, _):
-        v = u[s]
         p, g = s // groups, lax.rem(s, groups)
         after = pltpu.roll(landed[0, p], lax.rem(cz - g * SLOT, cz), 2)
         before = pltpu.roll(landed[1, p], cz - (g + 1) * SLOT, 2)
-        total = (2.0 * WEIGHTS[0]) * v
-        for d in range(1, REACH + 1):
-            up = pltpu.roll(jnp.where(lane < d, after, v), cz - d, 2)
-            down = pltpu.roll(jnp.where(lane >= cz - d, before, v), d, 2)
-            total = total + WEIGHTS[d] * (up + down)
-        acc[s] = total + rows_sum(v, own)
+        halo = jnp.where(lane < cz // 2, after, before)
+        acc[s] = acc[s] + along_lanes(halo.reshape(cx * cy, cz), across).reshape(cx, cy, cz)
         return 0
 
-    lax.fori_loop(0, species, along_z, 0)
+    each(0, species, AT_ONCE[2], along_z)
 
     def along_x(s, _):
         cells = [xl[s, i] for i in range(REACH)] + [u[s, i] for i in range(cx)]
@@ -218,12 +276,13 @@
         pl.when(odd)(go_on)
         pl.when(jnp.logical_not(odd))(pass_on)
 
+    for k, (begin, size) in enumerate(x_spans):
+        for copy in x_copies[k]:
+            copy.wait_recv()
+        lax.fori_loop(begin, begin + size, along_x, 0)
     for k, (begin, size) in enumerate(spans):
         if k == early:
             take_turn()
-        for copy in x_copies[k]:
-            copy.wait_recv()
-        lax.fori_loop(begin, begin + size, along_x, 0)
         for copy in y_copies[k]:
             copy.wait_recv()
         lax.fori_loop(begin, begin + size, along_y, 0)
@@ -242,13 +301,14 @@
     cuts = CUTS if sum(CUTS) == species else (1,) * species
     pieces = len(cuts)
     early = EARLY if sum(CUTS) == species and nx % 2 == 0 else pieces
+    x_size = species // X_PIECES if species % X_PIECES == 0 else 1
     sides = 1 if ny == 2 else 2
     groups = cz // SLOT
     rows_packed = -(-species // groups)
     block = (species, cx, cy, cz)
     dma = pltpu.SemaphoreType.DMA
     return pl.pallas_call(
-        functools.partial(kernel, nx, ny, nz, cuts, early),
+        functools.partial(kernel, nx, ny, nz, cuts, early, x_size),
         out_shape=pltpu.VMEM(block, jnp.float32),
         in_specs=[pl.BlockSpec(memory_space=pltpu.HBM), pl.BlockSpec(memory_space=pl.ANY)],
         out_specs=pl.BlockSpec(memory_space=pltpu.VMEM),
@@ -262,13 +322,13 @@
             pltpu.VMEM((2, rows_packed, cx, cy, cz), jnp.float32),
             pltpu.VMEM((2, rows_packed, cx, cy, cz), jnp.float32),
             dma((pieces + 1,)),
-            dma((2, pieces)),
-            dma((2, pieces)),
+            dma((2, species // x_size)),
+            dma((2, species // x_size)),
             dma((sides, pieces)),
             dma((sides, pieces)),
             dma((2,)),
             dma((2,)),
-            pltpu.SemaphoreType.REGULAR((4,)),
+            pltpu.SemaphoreType.REGULAR((5,)),
             pltpu.SemaphoreType.REGULAR,
         ],
         compiler_params=pltpu.CompilerParams(collective_id=0, has_side_effects=True, vmem_limit_bytes=56 * 1024 * 1024),

time: 32.3 us -> 27.9 us (0.86)
  Pallas kernels: 31.1 us -> 26.8 us
    pallas_call x1, Pallas kernels: 31.1 us -> 26.8 us  [local(): pl.pallas_call(functools.partial(kernel, nx, ny, nz, cuts, early, x_size)...]
where the time goes in v2:
time: 27.9 us; the launch traced here: 27.7 us
  Pallas kernels  26.8 us (96%)
  local copies, waits for them, and re-layouts  0.97 us (3%)
    pallas_call x1, Pallas kernels, local(): pl.pallas_call(functools.partial(kernel, nx, ny, nz, cuts, early, x_size)...  26.8 us
    unnamed x1, local copies, waits for them, and re-layouts  0.97 us

profile of v2, /device:TPU:1, one launch (start us, length us, event | category | flops | bytes accessed | tf_op | source)
XLA Modules:
  0.0 27.7 jit_solution(2143966526489065174)
XLA Ops:
  0.0 26.8 %filter_pass.1 = f32[32,8,8,128]{3,2,1,0:T(8,128)S(1)} custom-call(f32[32,8,8,128]{3,2,1,0:T(8,128)} %fields.1, f32[32]{0:T(128)} %strength_in.1), custom_call_target="tpu_custom_call" | custom-call | tf_op jit(solution)/shard_map/filter_pass/pallas_call | solution.py:310
  26.8 1.0 %copy.4 = f32[32,8,8,128]{3,2,1,0:T(8,128)} copy(f32[32,8,8,128]{3,2,1,0:T(8,128)S(1)} %filter_pass.1) | data formatting | bytes 2097152

commit v3 on v2

--- a/solution.py
+++ b/solution.py
@@ -10,9 +10,8 @@
 REACH = 5
 SLOT = 8
 WEIGHTS = [-252.0, 210.0, -120.0, 45.0, -10.0, 1.0]
-CUTS = (2, 8, 8, 6, 3, 2, 2, 1)
-EARLY = 4
-X_PIECES = 2
+CUTS = (1, 23, 3, 2, 2, 1)
+EARLY = 2
 AT_ONCE = (8, 4, 8)
 
 
@@ -74,7 +73,7 @@
     return total
 
 
-def kernel(nx, ny, nz, cuts, early, x_size, fields, strength_in, out, strength, u, acc, xl, xr, ys, packed, landed,
+def kernel(nx, ny, nz, cuts, early, fields, strength_in, out, strength, u, acc, xs, ys, packed, landed,
            in_sem, x_send, x_recv, y_send, y_recv, z_send, z_recv, answers, turn):
     species, cx, cy, cz = u.shape
     groups = cz // SLOT
@@ -104,70 +103,62 @@
     for size in cuts:
         spans.append((begin, size))
         begin += size
-    loads = []
-    for k, (begin, size) in enumerate(spans):
-        part = pl.ds(begin, size)
-        loads.append(pltpu.make_async_copy(fields.at[part], u.at[part], in_sem.at[k]))
-    gains = pltpu.make_async_copy(strength_in, strength, in_sem.at[len(cuts)])
+    head, rest = pl.ds(0, cuts[0]), pl.ds(cuts[0], species - cuts[0])
+    loads = [pltpu.make_async_copy(fields.at[part], u.at[part], in_sem.at[k]) for k, part in enumerate((head, rest))]
+    gains = pltpu.make_async_copy(strength_in, strength, in_sem.at[2])
     for load in loads:
         load.start()
     gains.start()
 
     held = early < len(cuts)
     odd = lax.rem(px, 2) == 1
-    y_copies, x_copies = [], []
+    mark = sum(cuts[:early + 1])
+    y_copies = []
     for k, (begin, size) in enumerate(spans):
         part = pl.ds(begin, size)
-        row = []
-        for side, peer in enumerate(y_peers):
-            row.append(pltpu.make_async_remote_copy(
+        y_copies.append([
+            pltpu.make_async_remote_copy(
                 src_ref=u.at[part], dst_ref=ys.at[side, part],
-                send_sem=y_send.at[side, k], recv_sem=y_recv.at[side, k],
-                device_id=(px, peer, pz), device_id_type=MESH))
-        y_copies.append(row)
-    x_spans = [(at, x_size) for at in range(0, species, x_size)]
-    for k, (begin, size) in enumerate(x_spans):
-        part = pl.ds(begin, size)
-        x_copies.append([
-            pltpu.make_async_remote_copy(
-                src_ref=u.at[part, pl.ds(cx - REACH, REACH)], dst_ref=xl.at[part],
-                send_sem=x_send.at[0, k], recv_sem=x_recv.at[0, k],
-                device_id=(x_right, py, pz), device_id_type=MESH),
-            pltpu.make_async_remote_copy(
-                src_ref=u.at[part, pl.ds(0, REACH)], dst_ref=xr.at[part],
-                send_sem=x_send.at[1, k], recv_sem=x_recv.at[1, k],
-                device_id=(x_left, py, pz), device_id_type=MESH),
-        ])
+                send_sem=y_send.at[side, int(begin >= mark)], recv_sem=y_recv.at[side, k],
+                device_id=(px, peer, pz), device_id_type=MESH)
+            for side, peer in enumerate(y_peers)])
+    x_copies = [
+        pltpu.make_async_remote_copy(
+            src_ref=u.at[:, pl.ds(begin, REACH)], dst_ref=xs.at[side],
+            send_sem=x_send, recv_sem=x_recv,
+            device_id=(peer, py, pz), device_id_type=MESH)
+        for side, (begin, peer) in enumerate(((cx - REACH, x_right), (0, x_left)))
+    ]
+
+    def settle(ref, semaphore):
+        pltpu.make_async_copy(ref, ref, semaphore).wait()
 
     def start_y(rows):
         for row in rows:
             for copy in row:
                 copy.start()
 
-    def sent_y(rows):
-        for row in rows:
-            for copy in row:
-                copy.wait_send()
+    def sent_y(group):
+        part = pl.ds(0, mark) if group == 0 else pl.ds(mark, species - mark)
+        for side in range(len(y_peers)):
+            settle(u.at[part], y_send.at[side, group])
 
     greeters = sum(c.astype(jnp.int32) for c in (px > 0, last_x, pz > 0))
     pl.semaphore_wait(barrier, len(y_peers) + greeters)
-    for load, row in zip(loads[:early], y_copies[:early]):
-        load.wait()
-        start_y([row])
-    for load in loads[early:]:
-        load.wait()
+    loads[0].wait()
+    start_y(y_copies[:1])
+    loads[1].wait()
+    start_y(y_copies[1:early])
     if held:
         pl.when(jnp.logical_not(odd))(lambda: start_y(y_copies[early:]))
     pl.when(px > 0)(lambda: tell(answers.at[0], left_x))
-    pl.when(last_x)(lambda: tell(answers.at[1], right_x))
-    pl.when(pz > 0)(lambda: tell(answers.at[2], to_left))
-    pl.when(last_z)(lambda: tell(answers.at[4], to_left))
+    pl.when(last_x)(lambda: tell(answers.at[0], right_x))
+    pl.when(pz > 0)(lambda: tell(answers.at[1], to_left))
+    pl.when(last_z)(lambda: tell(answers.at[2], to_left))
     gains.wait()
-    pl.when(px < nx - 1)(lambda: pl.semaphore_wait(answers.at[0], 1))
-    pl.when(first_x)(lambda: pl.semaphore_wait(answers.at[1], 1))
-    for row in x_copies:
-        for copy in row:
-            copy.start()
+    pl.when(px < nx - 1)(lambda: pl.semaphore_wait(answers.at[0], first_x.astype(jnp.int32) + 1))
+    for copy in x_copies:
+        copy.start()
 
     lane = lax.broadcasted_iota(jnp.int32, (cx, cy, cz), 2)
     slot = lane // SLOT
@@ -191,30 +182,30 @@
     z_copies = [
         pltpu.make_async_remote_copy(
             src_ref=packed.at[side], dst_ref=landed.at[side],
-            send_sem=z_send.at[side], recv_sem=z_recv.at[side],
+            send_sem=z_send, recv_sem=z_recv,
             device_id=(px, py, peer), device_id_type=MESH)
         for side, peer in enumerate((z_left, z_right))
     ]
 
     def start_right():
+        pl.semaphore_wait(answers.at[1], 1)
+        z_copies[1].start()
+
+    def pass_token():
         pl.semaphore_wait(answers.at[2], 1)
+        tell(answers.at[2], to_left)
+
+    def close_ring():
+        pl.semaphore_wait(answers.at[2], 1)
+        tell(answers.at[1], to_left)
+        z_copies[0].start()
+
+    def end_ring():
+        pl.semaphore_wait(answers.at[1], 1)
         z_copies[1].start()
 
-    def pass_token():
-        pl.semaphore_wait(answers.at[4], 1)
-        tell(answers.at[4], to_left)
-
-    def close_ring():
-        pl.semaphore_wait(answers.at[4], 1)
-        tell(answers.at[3], to_left)
-        z_copies[0].start()
-
-    def end_ring():
-        pl.semaphore_wait(answers.at[3], 1)
-        z_copies[1].start()
-
+    pl.when(pz < nz - 1)(start_right)
     pl.when(pz > 0)(z_copies[0].start)
-    pl.when(pz < nz - 1)(start_right)
     pl.when(jnp.logical_and(pz > 0, pz < nz - 1))(pass_token)
     pl.when(first_z)(close_ring)
 
@@ -234,8 +225,7 @@
 
     each(0, species, AT_ONCE[1], along_own)
     pl.when(last_z)(end_ring)
-    for copy in z_copies:
-        copy.wait()
+    settle(landed, z_recv)
 
     def along_z(s, _):
         p, g = s // groups, lax.rem(s, groups)
@@ -248,8 +238,8 @@
     each(0, species, AT_ONCE[2], along_z)
 
     def along_x(s, _):
-        cells = [xl[s, i] for i in range(REACH)] + [u[s, i] for i in range(cx)]
-        cells += [xr[s, i] for i in range(REACH)]
+        cells = [xs[0, s, i] for i in range(REACH)] + [u[s, i] for i in range(cx)]
+        cells += [xs[1, s, i] for i in range(REACH)]
         for i in range(cx):
             total = acc[s, i]
             for d in range(1, REACH + 1):
@@ -264,36 +254,31 @@
         out[s] = u[s] + (strength[s] * (1.0 / 1024.0)) * total
         return 0
 
-    def take_turn():
-        def pass_on():
-            sent_y(y_copies[:early + 1])
-            tell(turn, right_x)
-
+    settle(xs, x_recv)
+    lax.fori_loop(0, species, along_x, 0)
+    if held:
         def go_on():
             pl.semaphore_wait(turn, 1)
             start_y(y_copies[early:])
 
+        def pass_on():
+            sent_y(0)
+            tell(turn, right_x)
+
         pl.when(odd)(go_on)
         pl.when(jnp.logical_not(odd))(pass_on)
-
-    for k, (begin, size) in enumerate(x_spans):
-        for copy in x_copies[k]:
-            copy.wait_recv()
-        lax.fori_loop(begin, begin + size, along_x, 0)
     for k, (begin, size) in enumerate(spans):
-        if k == early:
-            take_turn()
         for copy in y_copies[k]:
             copy.wait_recv()
         lax.fori_loop(begin, begin + size, along_y, 0)
-    for row in x_copies:
-        for copy in row:
-            copy.wait_send()
+    settle(xs, x_send)
+    settle(packed, z_send)
     if held:
-        pl.when(odd)(lambda: sent_y(y_copies[:early + 1]))
-        sent_y(y_copies[early + 1:])
+        pl.when(odd)(lambda: sent_y(0))
     else:
-        sent_y(y_copies)
+        sent_y(0)
+    if mark < species:
+        sent_y(1)
 
 
 def local(nx, ny, nz, fields, strength):
@@ -301,14 +286,13 @@
     cuts = CUTS if sum(CUTS) == species else (1,) * species
     pieces = len(cuts)
     early = EARLY if sum(CUTS) == species and nx % 2 == 0 else pieces
-    x_size = species // X_PIECES if species % X_PIECES == 0 else 1
     sides = 1 if ny == 2 else 2
     groups = cz // SLOT
     rows_packed = -(-species // groups)
     block = (species, cx, cy, cz)
     dma = pltpu.SemaphoreType.DMA
     return pl.pallas_call(
-        functools.partial(kernel, nx, ny, nz, cuts, early, x_size),
+        functools.partial(kernel, nx, ny, nz, cuts, early),
         out_shape=pltpu.VMEM(block, jnp.float32),
         in_specs=[pl.BlockSpec(memory_space=pltpu.HBM), pl.BlockSpec(memory_space=pl.ANY)],
         out_specs=pl.BlockSpec(memory_space=pltpu.VMEM),
@@ -316,19 +300,18 @@
             pltpu.SMEM((species,), jnp.float32),
             pltpu.VMEM(block, jnp.float32),
             pltpu.VMEM(block, jnp.float32),
-            pltpu.VMEM((species, REACH, cy, cz), jnp.float32),
-            pltpu.VMEM((species, REACH, cy, cz), jnp.float32),
+            pltpu.VMEM((2, species, REACH, cy, cz), jnp.float32),
             pltpu.VMEM((sides,) + block, jnp.float32),
             pltpu.VMEM((2, rows_packed, cx, cy, cz), jnp.float32),
             pltpu.VMEM((2, rows_packed, cx, cy, cz), jnp.float32),
-            dma((pieces + 1,)),
-            dma((2, species // x_size)),
-            dma((2, species // x_size)),
+            dma((3,)),
+            dma,
+            dma,
+            dma((sides, 2)),
             dma((sides, pieces)),
-            dma((sides, pieces)),
-            dma((2,)),
-            dma((2,)),
-            pltpu.SemaphoreType.REGULAR((5,)),
+            dma,
+            dma,
+            pltpu.SemaphoreType.REGULAR((3,)),
             pltpu.SemaphoreType.REGULAR,
         ],
         compiler_params=pltpu.CompilerParams(collective_id=0, has_side_effects=True, vmem_limit_bytes=56 * 1024 * 1024),

time: 27.9 us -> 27.7 us (level)
  no operation moved by 1% of the time
where the time goes in v3:
time: 27.7 us; the launch traced here: 27.5 us
  Pallas kernels  26.6 us (96%)
  local copies, waits for them, and re-layouts  0.97 us (4%)
    pallas_call x1, Pallas kernels, local(): pl.pallas_call(functools.partial(kernel, nx, ny, nz, cuts, early), out_sh...  26.6 us
    unnamed x1, local copies, waits for them, and re-layouts  0.97 us

profile of v3, /device:TPU:1, one launch (start us, length us, event | category | flops | bytes accessed | tf_op | source)
XLA Modules:
  0.0 27.5 jit_solution(11700486518893236415)
XLA Ops:
  0.0 26.6 %filter_pass.1 = f32[32,8,8,128]{3,2,1,0:T(8,128)S(1)} custom-call(f32[32,8,8,128]{3,2,1,0:T(8,128)} %fields.1, f32[32]{0:T(128)} %strength_in.1), custom_call_target="tpu_custom_call" | custom-call | tf_op jit(solution)/shard_map/filter_pass/pallas_call | solution.py:294
  26.6 1.0 %copy.4 = f32[32,8,8,128]{3,2,1,0:T(8,128)} copy(f32[32,8,8,128]{3,2,1,0:T(8,128)S(1)} %filter_pass.1) | data formatting | bytes 2097152

commit v4 on v3

--- a/solution.py
+++ b/solution.py
@@ -10,8 +10,8 @@
 REACH = 5
 SLOT = 8
 WEIGHTS = [-252.0, 210.0, -120.0, 45.0, -10.0, 1.0]
-CUTS = (1, 23, 3, 2, 2, 1)
-EARLY = 2
+CUTS = (24, 3, 2, 2, 1)
+EARLY = 1
 AT_ONCE = (8, 4, 8)
 
 
@@ -87,15 +87,24 @@
     barrier = pltpu.get_barrier_semaphore()
     to_left, to_right = (px, py, z_left), (px, py, z_right)
     left_x, right_x = (x_left, py, pz), (x_right, py, pz)
-    first_x, last_x, first_z, last_z = px == 0, px == nx - 1, pz == 0, pz == nz - 1
+    first_z, last_z = pz == 0, pz == nz - 1
 
     def tell(semaphore, peer):
         pl.semaphore_signal(semaphore, inc=1, device_id=peer, device_id_type=MESH)
 
     for peer in y_peers:
         tell(barrier, (px, peer, pz))
-    pl.when(px < nx - 1)(lambda: tell(barrier, right_x))
-    pl.when(first_x)(lambda: tell(barrier, left_x))
+    odd = lax.rem(px, 2) == 1
+    paired = nx % 2 == 0
+
+    def both_x(semaphore):
+        tell(semaphore, left_x)
+        tell(semaphore, right_x)
+
+    if paired:
+        pl.when(odd)(lambda: both_x(barrier))
+    else:
+        both_x(barrier)
     pl.when(pz < nz - 1)(lambda: tell(barrier, to_right))
 
     spans = []
@@ -103,22 +112,19 @@
     for size in cuts:
         spans.append((begin, size))
         begin += size
-    head, rest = pl.ds(0, cuts[0]), pl.ds(cuts[0], species - cuts[0])
-    loads = [pltpu.make_async_copy(fields.at[part], u.at[part], in_sem.at[k]) for k, part in enumerate((head, rest))]
-    gains = pltpu.make_async_copy(strength_in, strength, in_sem.at[2])
-    for load in loads:
-        load.start()
+    load = pltpu.make_async_copy(fields, u, in_sem.at[0])
+    gains = pltpu.make_async_copy(strength_in, strength, in_sem.at[1])
+    load.start()
     gains.start()
 
     held = early < len(cuts)
-    odd = lax.rem(px, 2) == 1
     mark = sum(cuts[:early + 1])
     y_copies = []
     for k, (begin, size) in enumerate(spans):
         part = pl.ds(begin, size)
         y_copies.append([
             pltpu.make_async_remote_copy(
-                src_ref=u.at[part], dst_ref=ys.at[side, part],
+                src_ref=(fields if k < early else u).at[part], dst_ref=ys.at[side, part],
                 send_sem=y_send.at[side, int(begin >= mark)], recv_sem=y_recv.at[side, k],
                 device_id=(px, peer, pz), device_id_type=MESH)
             for side, peer in enumerate(y_peers)])
@@ -143,20 +149,19 @@
         for side in range(len(y_peers)):
             settle(u.at[part], y_send.at[side, group])
 
-    greeters = sum(c.astype(jnp.int32) for c in (px > 0, last_x, pz > 0))
+    greeters = (pz > 0).astype(jnp.int32) + (2 * (1 - lax.rem(px, 2)) if paired else 2)
     pl.semaphore_wait(barrier, len(y_peers) + greeters)
-    loads[0].wait()
-    start_y(y_copies[:1])
-    loads[1].wait()
-    start_y(y_copies[1:early])
+    start_y(y_copies[:early])
+    load.wait()
     if held:
         pl.when(jnp.logical_not(odd))(lambda: start_y(y_copies[early:]))
-    pl.when(px > 0)(lambda: tell(answers.at[0], left_x))
-    pl.when(last_x)(lambda: tell(answers.at[0], right_x))
+    if paired:
+        pl.when(jnp.logical_not(odd))(lambda: both_x(answers.at[0]))
     pl.when(pz > 0)(lambda: tell(answers.at[1], to_left))
     pl.when(last_z)(lambda: tell(answers.at[2], to_left))
     gains.wait()
-    pl.when(px < nx - 1)(lambda: pl.semaphore_wait(answers.at[0], first_x.astype(jnp.int32) + 1))
+    if paired:
+        pl.when(odd)(lambda: pl.semaphore_wait(answers.at[0], 2))
     for copy in x_copies:
         copy.start()
 
@@ -304,7 +309,7 @@
             pltpu.VMEM((sides,) + block, jnp.float32),
             pltpu.VMEM((2, rows_packed, cx, cy, cz), jnp.float32),
             pltpu.VMEM((2, rows_packed, cx, cy, cz), jnp.float32),
-            dma((3,)),
+            dma((2,)),
             dma,
             dma,
             dma((sides, 2)),

time: 27.7 us -> 27 us (0.975)
  Pallas kernels: 26.6 us -> 25.9 us
    pallas_call x1, Pallas kernels: 26.6 us -> 25.9 us  [local(): pl.pallas_call(functools.partial(kernel, nx, ny, nz, cuts, early), out_sh...]
where the time goes in v4:
time: 27 us; the launch traced here: 26.9 us
  Pallas kernels  25.9 us (96%)
  local copies, waits for them, and re-layouts  0.97 us (4%)
    pallas_call x1, Pallas kernels, local(): pl.pallas_call(functools.partial(kernel, nx, ny, nz, cuts, early), out_sh...  25.9 us
    unnamed x1, local copies, waits for them, and re-layouts  0.97 us

profile of v4, /device:TPU:1, one launch (start us, length us, event | category | flops | bytes accessed | tf_op | source)
XLA Modules:
  0.0 26.9 jit_solution(9994894592028090981)
XLA Ops:
  0.0 25.9 %filter_pass.1 = f32[32,8,8,128]{3,2,1,0:T(8,128)S(1)} custom-call(f32[32,8,8,128]{3,2,1,0:T(8,128)} %fields.1, f32[32]{0:T(128)} %strength_in.1), custom_call_target="tpu_custom_call" | custom-call | tf_op jit(solution)/shard_map/filter_pass/pallas_call | solution.py:299
  25.9 1.0 %copy.4 = f32[32,8,8,128]{3,2,1,0:T(8,128)} copy(f32[32,8,8,128]{3,2,1,0:T(8,128)S(1)} %filter_pass.1) | data formatting | bytes 2097152

commit v5 on v4

--- a/solution.py
+++ b/solution.py
@@ -10,8 +10,8 @@
 REACH = 5
 SLOT = 8
 WEIGHTS = [-252.0, 210.0, -120.0, 45.0, -10.0, 1.0]
-CUTS = (24, 3, 2, 2, 1)
-EARLY = 1
+CUTS = (23, 1, 3, 2, 2, 1)
+EARLY = 2
 AT_ONCE = (8, 4, 8)
 
 
@@ -73,8 +73,8 @@
     return total
 
 
-def kernel(nx, ny, nz, cuts, early, fields, strength_in, out, strength, u, acc, xs, ys, packed, landed,
-           in_sem, x_send, x_recv, y_send, y_recv, z_send, z_recv, answers, turn):
+def kernel(nx, ny, nz, cuts, early, fields, strength_in, out, strength, u, acc, xs, ys, packed, landed, via,
+           in_sem, x_send, x_recv, y_send, y_recv, z_send, z_recv, via_send, via_recv, answers, turn):
     species, cx, cy, cz = u.shape
     groups = cz // SLOT
     rows_packed = packed.shape[1]
@@ -136,6 +136,22 @@
         for side, (begin, peer) in enumerate(((cx - REACH, x_right), (0, x_left)))
     ]
 
+    relayed = held and ny == 2 and nz > 1
+    on_way = jnp.logical_and(px == 1, pz < 2)
+    source = jnp.logical_and(on_way, jnp.logical_and(py == 1, pz == 0))
+    relay_out = jnp.logical_and(on_way, jnp.logical_and(py == 1, pz == 1))
+    relay_back = jnp.logical_and(on_way, jnp.logical_and(py == 0, pz == 1))
+    detour = pl.ds(spans[early - 1][0], via.shape[0])
+    hop_out = pltpu.make_async_remote_copy(
+        src_ref=u.at[detour], dst_ref=via, send_sem=y_send.at[0, 0], recv_sem=via_recv,
+        device_id=to_right, device_id_type=MESH)
+    hop_over = pltpu.make_async_remote_copy(
+        src_ref=via, dst_ref=via, send_sem=via_send, recv_sem=via_recv,
+        device_id=(px, y_right, pz), device_id_type=MESH)
+    hop_back = pltpu.make_async_remote_copy(
+        src_ref=via, dst_ref=ys.at[0, detour], send_sem=via_send, recv_sem=y_recv.at[0, early - 1],
+        device_id=to_left, device_id_type=MESH)
+
     def settle(ref, semaphore):
         pltpu.make_async_copy(ref, ref, semaphore).wait()
 
@@ -151,7 +167,11 @@
 
     greeters = (pz > 0).astype(jnp.int32) + (2 * (1 - lax.rem(px, 2)) if paired else 2)
     pl.semaphore_wait(barrier, len(y_peers) + greeters)
-    start_y(y_copies[:early])
+    if relayed:
+        start_y(y_copies[:early - 1])
+        pl.when(jnp.logical_not(source))(lambda: start_y(y_copies[early - 1:early]))
+    else:
+        start_y(y_copies[:early])
     load.wait()
     if held:
         pl.when(jnp.logical_not(odd))(lambda: start_y(y_copies[early:]))
@@ -209,7 +229,13 @@
         pl.semaphore_wait(answers.at[1], 1)
         z_copies[1].start()
 
+    def forward(hop):
+        settle(via, via_recv)
+        hop.start()
+
     pl.when(pz < nz - 1)(start_right)
+    if relayed:
+        pl.when(source)(hop_out.start)
     pl.when(pz > 0)(z_copies[0].start)
     pl.when(jnp.logical_and(pz > 0, pz < nz - 1))(pass_token)
     pl.when(first_z)(close_ring)
@@ -241,6 +267,8 @@
         return 0
 
     each(0, species, AT_ONCE[2], along_z)
+    if relayed:
+        pl.when(relay_out)(lambda: forward(hop_over))
 
     def along_x(s, _):
         cells = [xs[0, s, i] for i in range(REACH)] + [u[s, i] for i in range(cx)]
@@ -272,12 +300,16 @@
 
         pl.when(odd)(go_on)
         pl.when(jnp.logical_not(odd))(pass_on)
+    if relayed:
+        pl.when(relay_back)(lambda: forward(hop_back))
     for k, (begin, size) in enumerate(spans):
         for copy in y_copies[k]:
             copy.wait_recv()
         lax.fori_loop(begin, begin + size, along_y, 0)
     settle(xs, x_send)
     settle(packed, z_send)
+    if relayed:
+        pl.when(jnp.logical_or(relay_out, relay_back))(lambda: settle(via, via_send))
     if held:
         pl.when(odd)(lambda: sent_y(0))
     else:
@@ -309,11 +341,14 @@
             pltpu.VMEM((sides,) + block, jnp.float32),
             pltpu.VMEM((2, rows_packed, cx, cy, cz), jnp.float32),
             pltpu.VMEM((2, rows_packed, cx, cy, cz), jnp.float32),
+            pltpu.VMEM((cuts[early - 1], cx, cy, cz), jnp.float32),
             dma((2,)),
             dma,
             dma,
             dma((sides, 2)),
             dma((sides, pieces)),
+            dma,
+            dma,
             dma,
             dma,
             pltpu.SemaphoreType.REGULAR((3,)),

time: 27 us -> 26.8 us (level)
  Pallas kernels: 25.9 us -> 25.6 us
    pallas_call x1, Pallas kernels: 25.9 us -> 25.6 us  [local(): pl.pallas_call(functools.partial(kernel, nx, ny, nz, cuts, early), out_sh...]
where the time goes in v5:
time: 26.8 us; the launch traced here: 26.6 us
  Pallas kernels  25.6 us (96%)
  local copies, waits for them, and re-layouts  0.97 us (4%)
    pallas_call x1, Pallas kernels, local(): pl.pallas_call(functools.partial(kernel, nx, ny, nz, cuts, early), out_sh...  25.6 us
    unnamed x1, local copies, waits for them, and re-layouts  0.97 us

profile of v5, /device:TPU:1, one launch (start us, length us, event | category | flops | bytes accessed | tf_op | source)
XLA Modules:
  0.0 26.6 jit_solution(3955092275134140136)
XLA Ops:
  0.0 25.6 %filter_pass.1 = f32[32,8,8,128]{3,2,1,0:T(8,128)S(1)} custom-call(f32[32,8,8,128]{3,2,1,0:T(8,128)} %fields.1, f32[32]{0:T(128)} %strength_in.1), custom_call_target="tpu_custom_call" | custom-call | tf_op jit(solution)/shard_map/filter_pass/pallas_call | solution.py:331
  25.6 1.0 %copy.4 = f32[32,8,8,128]{3,2,1,0:T(8,128)} copy(f32[32,8,8,128]{3,2,1,0:T(8,128)S(1)} %filter_pass.1) | data formatting | bytes 2097152

commit v6 on v4

--- a/solution.py
+++ b/solution.py
@@ -10,8 +10,9 @@
 REACH = 5
 SLOT = 8
 WEIGHTS = [-252.0, 210.0, -120.0, 45.0, -10.0, 1.0]
-CUTS = (24, 3, 2, 2, 1)
-EARLY = 1
+CUTS = (19, 5, 7, 1)
+EARLY = 2
+DETOUR = 1
 AT_ONCE = (8, 4, 8)
 
 
@@ -73,8 +74,8 @@
     return total
 
 
-def kernel(nx, ny, nz, cuts, early, fields, strength_in, out, strength, u, acc, xs, ys, packed, landed,
-           in_sem, x_send, x_recv, y_send, y_recv, z_send, z_recv, answers, turn):
+def kernel(nx, ny, nz, cuts, early, fields, strength_in, out, strength, u, acc, tiles, xs, ys, packed, landed, via,
+           in_sem, sent, x_recv, y_send, y_recv, z_recv, via_recv, answers, turn):
     species, cx, cy, cz = u.shape
     groups = cz // SLOT
     rows_packed = packed.shape[1]
@@ -112,29 +113,52 @@
     for size in cuts:
         spans.append((begin, size))
         begin += size
-    load = pltpu.make_async_copy(fields, u, in_sem.at[0])
-    gains = pltpu.make_async_copy(strength_in, strength, in_sem.at[1])
+    load = pltpu.make_async_copy(fields, u, in_sem)
+    gains = pltpu.make_async_copy(strength_in, strength, in_sem)
     load.start()
-    gains.start()
 
     held = early < len(cuts)
-    mark = sum(cuts[:early + 1])
+    mark = sum(cuts[:early])
+    arrivals = [(0, mark)] + spans[early:]
     y_copies = []
     for k, (begin, size) in enumerate(spans):
         part = pl.ds(begin, size)
         y_copies.append([
             pltpu.make_async_remote_copy(
                 src_ref=(fields if k < early else u).at[part], dst_ref=ys.at[side, part],
-                send_sem=y_send.at[side, int(begin >= mark)], recv_sem=y_recv.at[side, k],
+                send_sem=y_send.at[side] if k < early else sent, recv_sem=y_recv.at[side, max(k - early + 1, 0)],
                 device_id=(px, peer, pz), device_id_type=MESH)
             for side, peer in enumerate(y_peers)])
     x_copies = [
         pltpu.make_async_remote_copy(
             src_ref=u.at[:, pl.ds(begin, REACH)], dst_ref=xs.at[side],
-            send_sem=x_send, recv_sem=x_recv,
+            send_sem=sent, recv_sem=x_recv,
             device_id=(peer, py, pz), device_id_type=MESH)
         for side, (begin, peer) in enumerate(((cx - REACH, x_right), (0, x_left)))
     ]
+
+    relayed = held and ny == 2 and nz > 1 and nx > 2 and cx > 2 * via.shape[1]
+    by_z, by_x = jnp.logical_and(px == 1, pz == 1), jnp.logical_and(px == 2, pz == 0)
+    upper = py == 1
+    source = jnp.logical_and(upper, jnp.logical_and(px == 1, pz == 0))
+    relay = jnp.logical_or(by_z, by_x)
+    relay_out = jnp.logical_and(upper, relay)
+    back_z, back_x = jnp.logical_and(py == 0, by_z), jnp.logical_and(py == 0, by_x)
+    turned, thick = pl.ds(*spans[early - 1]), via.shape[1]
+    over_z, over_x, straight = pl.ds(0, thick), pl.ds(thick, thick), pl.ds(2 * thick, cx - 2 * thick)
+
+    def hop(src, dst, send_sem, recv_sem, peer):
+        return pltpu.make_async_remote_copy(
+            src_ref=src, dst_ref=dst, send_sem=send_sem, recv_sem=recv_sem, device_id=peer, device_id_type=MESH)
+
+    if relayed:
+        across_y = (px, y_right, pz)
+        direct = hop(fields.at[turned, straight], ys.at[0, turned, straight], y_send.at[0], y_recv.at[0, 0], across_y)
+        out_z = hop(u.at[turned, over_z], via, y_send.at[0], via_recv, to_right)
+        out_x = hop(u.at[turned, over_x], via, y_send.at[0], via_recv, right_x)
+        over = hop(via, via, sent, via_recv, across_y)
+        home_z = hop(via, ys.at[0, turned, over_z], sent, y_recv.at[0, 0], to_left)
+        home_x = hop(via, ys.at[0, turned, over_x], sent, y_recv.at[0, 0], left_x)
 
     def settle(ref, semaphore):
         pltpu.make_async_copy(ref, ref, semaphore).wait()
@@ -144,24 +168,31 @@
             for copy in row:
                 copy.start()
 
-    def sent_y(group):
-        part = pl.ds(0, mark) if group == 0 else pl.ds(mark, species - mark)
+    def early_sent():
         for side in range(len(y_peers)):
-            settle(u.at[part], y_send.at[side, group])
+            settle(u.at[pl.ds(0, mark)], y_send.at[side])
 
     greeters = (pz > 0).astype(jnp.int32) + (2 * (1 - lax.rem(px, 2)) if paired else 2)
     pl.semaphore_wait(barrier, len(y_peers) + greeters)
-    start_y(y_copies[:early])
+    if relayed:
+        start_y(y_copies[:early - 1])
+        pl.when(source)(direct.start)
+        pl.when(jnp.logical_not(source))(lambda: start_y(y_copies[early - 1:early]))
+    else:
+        start_y(y_copies[:early])
     load.wait()
+    gains.start()
     if held:
-        pl.when(jnp.logical_not(odd))(lambda: start_y(y_copies[early:]))
+        at_once = jnp.logical_not(jnp.logical_or(odd, relay_out) if relayed else odd)
+        pl.when(at_once)(lambda: start_y(y_copies[early:]))
     if paired:
         pl.when(jnp.logical_not(odd))(lambda: both_x(answers.at[0]))
     pl.when(pz > 0)(lambda: tell(answers.at[1], to_left))
     pl.when(last_z)(lambda: tell(answers.at[2], to_left))
-    gains.wait()
     if paired:
         pl.when(odd)(lambda: pl.semaphore_wait(answers.at[0], 2))
+    if relayed:
+        pl.when(source)(out_x.start)
     for copy in x_copies:
         copy.start()
 
@@ -187,10 +218,12 @@
     z_copies = [
         pltpu.make_async_remote_copy(
             src_ref=packed.at[side], dst_ref=landed.at[side],
-            send_sem=z_send, recv_sem=z_recv,
+            send_sem=sent, recv_sem=z_recv,
             device_id=(px, py, peer), device_id_type=MESH)
         for side, peer in enumerate((z_left, z_right))
     ]
+
+    gains.wait()
 
     def start_right():
         pl.semaphore_wait(answers.at[1], 1)
@@ -209,7 +242,13 @@
         pl.semaphore_wait(answers.at[1], 1)
         z_copies[1].start()
 
+    def forward(hop):
+        settle(via, via_recv)
+        hop.start()
+
     pl.when(pz < nz - 1)(start_right)
+    if relayed:
+        pl.when(source)(out_z.start)
     pl.when(pz > 0)(z_copies[0].start)
     pl.when(jnp.logical_and(pz > 0, pz < nz - 1))(pass_token)
     pl.when(first_z)(close_ring)
@@ -241,6 +280,12 @@
         return 0
 
     each(0, species, AT_ONCE[2], along_z)
+    if relayed:
+        def forward_out():
+            forward(over)
+            pl.when(jnp.logical_not(odd))(lambda: start_y(y_copies[early:]))
+
+        pl.when(relay_out)(forward_out)
 
     def along_x(s, _):
         cells = [xs[0, s, i] for i in range(REACH)] + [u[s, i] for i in range(cx)]
@@ -259,31 +304,38 @@
         out[s] = u[s] + (strength[s] * (1.0 / 1024.0)) * total
         return 0
 
+    def go_on():
+        pl.semaphore_wait(turn, 1)
+        start_y(y_copies[early:])
+
+    def pass_on():
+        early_sent()
+        tell(turn, right_x)
+
+    if held:
+        pl.when(jnp.logical_not(odd))(pass_on)
+    if relayed:
+        pl.when(back_x)(lambda: forward(home_x))
     settle(xs, x_recv)
     lax.fori_loop(0, species, along_x, 0)
     if held:
-        def go_on():
-            pl.semaphore_wait(turn, 1)
-            start_y(y_copies[early:])
-
-        def pass_on():
-            sent_y(0)
-            tell(turn, right_x)
-
         pl.when(odd)(go_on)
-        pl.when(jnp.logical_not(odd))(pass_on)
-    for k, (begin, size) in enumerate(spans):
-        for copy in y_copies[k]:
-            copy.wait_recv()
+    if relayed:
+        pl.when(back_z)(lambda: forward(home_z))
+    for k, (begin, size) in enumerate(arrivals):
+        for side in range(len(y_peers)):
+            settle(ys.at[side, pl.ds(begin, size)], y_recv.at[side, k])
         lax.fori_loop(begin, begin + size, along_y, 0)
-    settle(xs, x_send)
-    settle(packed, z_send)
     if held:
-        pl.when(odd)(lambda: sent_y(0))
-    else:
-        sent_y(0)
-    if mark < species:
-        sent_y(1)
+        pl.when(odd)(early_sent)
+    else:
+        early_sent()
+    layers = 2 * species * REACH + 2 * rows_packed * cx + len(y_peers) * (species - mark) * cx
+    if relayed:
+        pl.when(relay)(lambda: settle(tiles.at[pl.ds(0, layers + via.shape[0] * thick)], sent))
+        pl.when(jnp.logical_not(relay))(lambda: settle(tiles.at[pl.ds(0, layers)], sent))
+    else:
+        settle(tiles.at[pl.ds(0, layers)], sent)
 
 
 def local(nx, ny, nz, fields, strength):
@@ -295,6 +347,7 @@
     groups = cz // SLOT
     rows_packed = -(-species // groups)
     block = (species, cx, cy, cz)
+    layers = 2 * species * REACH + 2 * rows_packed * cx + sides * species * cx + species * DETOUR
     dma = pltpu.SemaphoreType.DMA
     return pl.pallas_call(
         functools.partial(kernel, nx, ny, nz, cuts, early),
@@ -305,15 +358,17 @@
             pltpu.SMEM((species,), jnp.float32),
             pltpu.VMEM(block, jnp.float32),
             pltpu.VMEM(block, jnp.float32),
+            pltpu.VMEM((layers, cy, cz), jnp.float32),
             pltpu.VMEM((2, species, REACH, cy, cz), jnp.float32),
             pltpu.VMEM((sides,) + block, jnp.float32),
             pltpu.VMEM((2, rows_packed, cx, cy, cz), jnp.float32),
             pltpu.VMEM((2, rows_packed, cx, cy, cz), jnp.float32),
-            dma((2,)),
-            dma,
-            dma,
-            dma((sides, 2)),
-            dma((sides, pieces)),
+            pltpu.VMEM((cuts[early - 1], DETOUR, cy, cz), jnp.float32),
+            dma,
+            dma,
+            dma,
+            dma((sides,)),
+            dma((sides, pieces - early + 1)),
             dma,
             dma,
             pltpu.SemaphoreType.REGULAR((3,)),

time: 27 us -> 26.6 us (0.985)
  Pallas kernels: 25.9 us -> 25.4 us
    pallas_call x1, Pallas kernels: 25.9 us -> 25.4 us  [local(): pl.pallas_call(functools.partial(kernel, nx, ny, nz, cuts, early), out_sh...]
where the time goes in v6:
time: 26.6 us; the launch traced here: 26.4 us
  Pallas kernels  25.4 us (95%)
  local copies, waits for them, and re-layouts  0.97 us (4%)
    pallas_call x1, Pallas kernels, local(): pl.pallas_call(functools.partial(kernel, nx, ny, nz, cuts, early), out_sh...  25.4 us
    unnamed x1, local copies, waits for them, and re-layouts  0.97 us

profile of v6, /device:TPU:1, one launch (start us, length us, event | category | flops | bytes accessed | tf_op | source)
XLA Modules:
  0.0 26.4 jit_solution(14791066254598887666)
XLA Ops:
  0.0 25.4 %filter_pass.1 = f32[32,8,8,128]{3,2,1,0:T(8,128)S(1)} custom-call(f32[32,8,8,128]{3,2,1,0:T(8,128)} %fields.1, f32[32]{0:T(128)} %strength_in.1), custom_call_target="tpu_custom_call" | custom-call | tf_op jit(solution)/shard_map/filter_pass/pallas_call | solution.py:352
  25.4 1.0 %copy.4 = f32[32,8,8,128]{3,2,1,0:T(8,128)} copy(f32[32,8,8,128]{3,2,1,0:T(8,128)S(1)} %filter_pass.1) | data formatting | bytes 2097152

commit v7 on v6

--- a/solution.py
+++ b/solution.py
@@ -119,14 +119,13 @@
 
     held = early < len(cuts)
     mark = sum(cuts[:early])
-    arrivals = [(0, mark)] + spans[early:]
     y_copies = []
     for k, (begin, size) in enumerate(spans):
         part = pl.ds(begin, size)
         y_copies.append([
             pltpu.make_async_remote_copy(
                 src_ref=(fields if k < early else u).at[part], dst_ref=ys.at[side, part],
-                send_sem=y_send.at[side] if k < early else sent, recv_sem=y_recv.at[side, max(k - early + 1, 0)],
+                send_sem=y_send.at[side] if k < early else sent, recv_sem=y_recv.at[side, k],
                 device_id=(px, peer, pz), device_id_type=MESH)
             for side, peer in enumerate(y_peers)])
     x_copies = [
@@ -153,12 +152,12 @@
 
     if relayed:
         across_y = (px, y_right, pz)
-        direct = hop(fields.at[turned, straight], ys.at[0, turned, straight], y_send.at[0], y_recv.at[0, 0], across_y)
+        direct = hop(fields.at[turned, straight], ys.at[0, turned, straight], y_send.at[0], y_recv.at[0, early - 1], across_y)
         out_z = hop(u.at[turned, over_z], via, y_send.at[0], via_recv, to_right)
         out_x = hop(u.at[turned, over_x], via, y_send.at[0], via_recv, right_x)
         over = hop(via, via, sent, via_recv, across_y)
-        home_z = hop(via, ys.at[0, turned, over_z], sent, y_recv.at[0, 0], to_left)
-        home_x = hop(via, ys.at[0, turned, over_x], sent, y_recv.at[0, 0], left_x)
+        home_z = hop(via, ys.at[0, turned, over_z], sent, y_recv.at[0, early - 1], to_left)
+        home_x = hop(via, ys.at[0, turned, over_x], sent, y_recv.at[0, early - 1], left_x)
 
     def settle(ref, semaphore):
         pltpu.make_async_copy(ref, ref, semaphore).wait()
@@ -322,7 +321,7 @@
         pl.when(odd)(go_on)
     if relayed:
         pl.when(back_z)(lambda: forward(home_z))
-    for k, (begin, size) in enumerate(arrivals):
+    for k, (begin, size) in enumerate(spans):
         for side in range(len(y_peers)):
             settle(ys.at[side, pl.ds(begin, size)], y_recv.at[side, k])
         lax.fori_loop(begin, begin + size, along_y, 0)
@@ -368,7 +367,7 @@
             dma,
             dma,
             dma((sides,)),
-            dma((sides, pieces - early + 1)),
+            dma((sides, pieces)),
             dma,
             dma,
             pltpu.SemaphoreType.REGULAR((3,)),

time: 26.6 us -> 26.6 us (level)
  no operation moved by 1% of the time
where the time goes in v7:
time: 26.6 us; the launch traced here: 26.4 us
  Pallas kernels  25.4 us (95%)
  local copies, waits for them, and re-layouts  0.97 us (4%)
    pallas_call x1, Pallas kernels, local(): pl.pallas_call(functools.partial(kernel, nx, ny, nz, cuts, early), out_sh...  25.4 us
    unnamed x1, local copies, waits for them, and re-layouts  0.97 us

profile of v7, /device:TPU:1, one launch (start us, length us, event | category | flops | bytes accessed | tf_op | source)
XLA Modules:
  0.0 26.4 jit_solution(4003364570236044984)
XLA Ops:
  0.0 25.4 %filter_pass.1 = f32[32,8,8,128]{3,2,1,0:T(8,128)S(1)} custom-call(f32[32,8,8,128]{3,2,1,0:T(8,128)} %fields.1, f32[32]{0:T(128)} %strength_in.1), custom_call_target="tpu_custom_call" | custom-call | tf_op jit(solution)/shard_map/filter_pass/pallas_call | solution.py:351
  25.5 1.0 %copy.4 = f32[32,8,8,128]{3,2,1,0:T(8,128)} copy(f32[32,8,8,128]{3,2,1,0:T(8,128)S(1)} %filter_pass.1) | data formatting | bytes 2097152

commit v8 on v4

--- a/solution.py
+++ b/solution.py
@@ -10,8 +10,9 @@
 REACH = 5
 SLOT = 8
 WEIGHTS = [-252.0, 210.0, -120.0, 45.0, -10.0, 1.0]
-CUTS = (24, 3, 2, 2, 1)
-EARLY = 1
+CUTS = (16, 5, 3, 2, 5, 1)
+EARLY = 2
+LATE = 2
 AT_ONCE = (8, 4, 8)
 
 
@@ -73,8 +74,8 @@
     return total
 
 
-def kernel(nx, ny, nz, cuts, early, fields, strength_in, out, strength, u, acc, xs, ys, packed, landed,
-           in_sem, x_send, x_recv, y_send, y_recv, z_send, z_recv, answers, turn):
+def kernel(nx, ny, nz, cuts, early, late, fields, strength_in, out, late_u, late_gain, strength, u, acc, tiles, xs, ys, packed, landed,
+           in_sem, sent, x_recv, y_send, y_recv, z_recv, answers, turn):
     species, cx, cy, cz = u.shape
     groups = cz // SLOT
     rows_packed = packed.shape[1]
@@ -112,27 +113,30 @@
     for size in cuts:
         spans.append((begin, size))
         begin += size
-    load = pltpu.make_async_copy(fields, u, in_sem.at[0])
-    gains = pltpu.make_async_copy(strength_in, strength, in_sem.at[1])
+    load = pltpu.make_async_copy(fields, u, in_sem)
+    late_load = pltpu.make_async_copy(fields.at[pl.ds(species - late, late)], late_u, in_sem) if late else None
+    gains = pltpu.make_async_copy(strength_in, strength, in_sem)
     load.start()
-    gains.start()
 
     held = early < len(cuts)
     mark = sum(cuts[:early + 1])
+    kept = species - late
     y_copies = []
     for k, (begin, size) in enumerate(spans):
         part = pl.ds(begin, size)
         y_copies.append([
             pltpu.make_async_remote_copy(
                 src_ref=(fields if k < early else u).at[part], dst_ref=ys.at[side, part],
-                send_sem=y_send.at[side, int(begin >= mark)], recv_sem=y_recv.at[side, k],
+                send_sem=y_send.at[side] if begin < mark else sent, recv_sem=y_recv.at[side, k],
                 device_id=(px, peer, pz), device_id_type=MESH)
             for side, peer in enumerate(y_peers)])
+    x_spans = [(0, cuts[0]), (cuts[0], species - cuts[0])]
     x_copies = [
         pltpu.make_async_remote_copy(
-            src_ref=u.at[:, pl.ds(begin, REACH)], dst_ref=xs.at[side],
-            send_sem=x_send, recv_sem=x_recv,
+            src_ref=u.at[pl.ds(*span), pl.ds(begin, REACH)], dst_ref=xs.at[pl.ds(*span), side],
+            send_sem=sent, recv_sem=x_recv.at[k],
             device_id=(peer, py, pz), device_id_type=MESH)
+        for k, span in enumerate(x_spans)
         for side, (begin, peer) in enumerate(((cx - REACH, x_right), (0, x_left)))
     ]
 
@@ -144,26 +148,29 @@
             for copy in row:
                 copy.start()
 
-    def sent_y(group):
-        part = pl.ds(0, mark) if group == 0 else pl.ds(mark, species - mark)
+    def early_sent():
         for side in range(len(y_peers)):
-            settle(u.at[part], y_send.at[side, group])
+            settle(u.at[pl.ds(0, mark)], y_send.at[side])
 
     greeters = (pz > 0).astype(jnp.int32) + (2 * (1 - lax.rem(px, 2)) if paired else 2)
     pl.semaphore_wait(barrier, len(y_peers) + greeters)
     start_y(y_copies[:early])
     load.wait()
+    gains.start()
     if held:
-        pl.when(jnp.logical_not(odd))(lambda: start_y(y_copies[early:]))
+        pl.when(odd)(lambda: start_y(y_copies[early:-LATE]))
     if paired:
         pl.when(jnp.logical_not(odd))(lambda: both_x(answers.at[0]))
     pl.when(pz > 0)(lambda: tell(answers.at[1], to_left))
     pl.when(last_z)(lambda: tell(answers.at[2], to_left))
-    gains.wait()
     if paired:
         pl.when(odd)(lambda: pl.semaphore_wait(answers.at[0], 2))
-    for copy in x_copies:
-        copy.start()
+    for k in range(0, len(x_copies), 2):
+        if held:
+            pl.when(jnp.logical_not(odd))(x_copies[k].start)
+        else:
+            x_copies[k].start()
+        x_copies[k + 1].start()
 
     lane = lax.broadcasted_iota(jnp.int32, (cx, cy, cz), 2)
     slot = lane // SLOT
@@ -187,10 +194,16 @@
     z_copies = [
         pltpu.make_async_remote_copy(
             src_ref=packed.at[side], dst_ref=landed.at[side],
-            send_sem=z_send, recv_sem=z_recv,
+            send_sem=sent, recv_sem=z_recv,
             device_id=(px, py, peer), device_id_type=MESH)
         for side, peer in enumerate((z_left, z_right))
     ]
+
+    gains.wait()
+    if held:
+        late_load.start()
+        for i in range(late):
+            late_gain[i] = jnp.zeros((cy, cz), jnp.float32) + strength[kept + i] * (1.0 / 1024.0)
 
     def start_right():
         pl.semaphore_wait(answers.at[1], 1)
@@ -229,6 +242,12 @@
         return 0
 
     each(0, species, AT_ONCE[1], along_own)
+    if held:
+        def start_held():
+            for copy in x_copies[0::2]:
+                copy.start()
+
+        pl.when(odd)(start_held)
     pl.when(last_z)(end_ring)
     settle(landed, z_recv)
 
@@ -243,47 +262,155 @@
     each(0, species, AT_ONCE[2], along_z)
 
     def along_x(s, _):
-        cells = [xs[0, s, i] for i in range(REACH)] + [u[s, i] for i in range(cx)]
-        cells += [xs[1, s, i] for i in range(REACH)]
+        gain = strength[s] * (1.0 / 1024.0)
+        cells = [xs[s, 0, i] for i in range(REACH)] + [u[s, i] for i in range(cx)]
+        cells += [xs[s, 1, i] for i in range(REACH)]
         for i in range(cx):
             total = acc[s, i]
             for d in range(1, REACH + 1):
                 total = total + WEIGHTS[d] * (cells[REACH + i - d] + cells[REACH + i + d])
             acc[s, i] = total
+            out[s, i] = cells[REACH + i] + gain * total
         return 0
 
-    def along_y(s, _):
+    def from_y(s):
         total = acc[s]
         for side, weights in enumerate(remote):
             total = total + rows_sum(ys[side, s], weights)
-        out[s] = u[s] + (strength[s] * (1.0 / 1024.0)) * total
+        return total
+
+    def along_y(s, _):
+        acc[s] = from_y(s)
         return 0
 
-    settle(xs, x_recv)
-    lax.fori_loop(0, species, along_x, 0)
+    def along_last(s, _):
+        out[s] = u[s] + (strength[s] * (1.0 / 1024.0)) * from_y(s)
+        return 0
+
+    def go_on():
+        pl.semaphore_wait(turn, 1)
+        start_y(y_copies[early:])
+
+    def pass_on():
+        early_sent()
+        tell(turn, left_x)
+
+    def add_y(k, body):
+        begin, size = spans[k]
+        for side in range(len(y_peers)):
+            settle(ys.at[side, pl.ds(begin, size)], y_recv.at[side, k])
+        lax.fori_loop(begin, begin + size, body, 0)
+
+    def add_x(k):
+        begin, size = x_spans[k]
+        settle(xs.at[pl.ds(begin, size)], x_recv.at[k])
+        lax.fori_loop(begin, begin + size, along_x, 0)
+
+    def rest():
+        for k in range(len(spans) - LATE, len(spans)):
+            add_y(k, along_last)
+
+    add_y(0, along_y)
+    add_x(0)
     if held:
-        def go_on():
-            pl.semaphore_wait(turn, 1)
-            start_y(y_copies[early:])
-
-        def pass_on():
-            sent_y(0)
-            tell(turn, right_x)
-
-        pl.when(odd)(go_on)
-        pl.when(jnp.logical_not(odd))(pass_on)
-    for k, (begin, size) in enumerate(spans):
-        for copy in y_copies[k]:
-            copy.wait_recv()
-        lax.fori_loop(begin, begin + size, along_y, 0)
-    settle(xs, x_send)
-    settle(packed, z_send)
+        pl.when(odd)(pass_on)
+        pl.when(jnp.logical_not(odd))(go_on)
+        for k in range(1, early + 1):
+            add_y(k, along_y)
+        add_x(1)
+        for k in range(early + 1, len(spans) - LATE):
+            add_y(k, along_last)
+        late_load.wait()
+        pl.when(jnp.logical_not(odd))(rest)
+        pl.when(jnp.logical_not(odd))(early_sent)
+    else:
+        add_x(1)
+        for k in range(1, len(spans)):
+            add_y(k, along_last)
+        early_sent()
+    layers = 2 * species * REACH + 2 * rows_packed * cx
+    tails = [(None, 0)]
     if held:
-        pl.when(odd)(lambda: sent_y(0))
-    else:
-        sent_y(0)
-    if mark < species:
-        sent_y(1)
+        sides = len(y_peers)
+        tails = [(odd, sides * (kept - mark) * cx), (jnp.logical_not(odd), sides * (species - mark) * cx)]
+    for who, count in tails:
+        last = functools.partial(settle, tiles.at[pl.ds(0, layers + count)], sent)
+        if who is None:
+            last()
+        else:
+            pl.when(who)(last)
+
+
+def late_kernel(ny, cuts, filtered, late_u, late_gain, _, late_out, ys, send, recv):
+    late, cx, cy, cz = late_u.shape
+    px, py, pz = lax.axis_index("gx"), lax.axis_index("gy"), lax.axis_index("gz")
+    y_left, y_right = lax.rem(py + ny - 1, ny), lax.rem(py + 1, ny)
+    y_peers = [y_right] if ny == 2 else [y_right, y_left]
+    kept = filtered.shape[0] - late
+
+    def exchange():
+        barrier = pltpu.get_barrier_semaphore()
+        for peer in y_peers:
+            pl.semaphore_signal(barrier, inc=1, device_id=(px, peer, pz), device_id_type=MESH)
+        pl.semaphore_wait(barrier, len(y_peers))
+        copies = []
+        begin = 0
+        for k, size in enumerate(cuts):
+            part = pl.ds(begin, size)
+            copies.append([
+                pltpu.make_async_remote_copy(
+                    src_ref=late_u.at[part], dst_ref=ys.at[side, part], send_sem=send.at[side], recv_sem=recv.at[side, k],
+                    device_id=(px, peer, pz), device_id_type=MESH)
+                for side, peer in enumerate(y_peers)])
+            begin += size
+        for row in copies:
+            for copy in row:
+                copy.start()
+        if ny == 2:
+            remote = [[row_weights(cy, cz, r, (cy, -cy)) for r in range(cy)]]
+        else:
+            remote = [[row_weights(cy, cz, r, (base,)) for r in range(cy)] for base in (-cy, cy)]
+        s = 0
+        for size, row in zip(cuts, copies):
+            for copy in row:
+                copy.wait_recv()
+            for s in range(s, s + size):
+                total = None
+                for side, weights in enumerate(remote):
+                    term = rows_sum(ys[side, s], weights)
+                    total = term if total is None else total + term
+                late_out[s] = filtered[kept + s] + late_gain[s][None] * total
+            s += 1
+        for side in range(len(y_peers)):
+            pltpu.make_async_copy(late_u, late_u, send.at[side]).wait()
+
+    pl.when(lax.rem(px, 2) == 1)(exchange)
+
+
+def write_kernel(late, filtered, out, token, done):
+    species = filtered.shape[0]
+
+    def write(count):
+        part = pl.ds(0, count)
+        copy = pltpu.make_async_copy(filtered.at[part], out.at[part], done)
+        copy.start()
+        copy.wait()
+
+    odd = lax.rem(lax.axis_index("gx"), 2) == 1
+    pl.when(odd)(lambda: write(species - late))
+    pl.when(jnp.logical_not(odd))(lambda: write(species))
+    token[...] = jnp.zeros(token.shape, token.dtype)
+
+
+def close_kernel(_, late_out, out, done):
+    late, species = late_out.shape[0], out.shape[0]
+
+    def write():
+        copy = pltpu.make_async_copy(late_out, out.at[pl.ds(species - late, late)], done)
+        copy.start()
+        copy.wait()
+
+    pl.when(lax.rem(lax.axis_index("gx"), 2) == 1)(write)
 
 
 def local(nx, ny, nz, fields, strength):
@@ -295,26 +422,29 @@
     groups = cz // SLOT
     rows_packed = -(-species // groups)
     block = (species, cx, cy, cz)
+    layers = 2 * species * REACH + 2 * rows_packed * cx + sides * species * cx
     dma = pltpu.SemaphoreType.DMA
-    return pl.pallas_call(
-        functools.partial(kernel, nx, ny, nz, cuts, early),
-        out_shape=pltpu.VMEM(block, jnp.float32),
+    late = sum(cuts[-LATE:])
+    filtered, late_u, late_gain = pl.pallas_call(
+        functools.partial(kernel, nx, ny, nz, cuts, early, late),
+        out_shape=(pltpu.VMEM(block, jnp.float32), pltpu.VMEM((late,) + block[1:], jnp.float32),
+                   pltpu.VMEM((late, cy, cz), jnp.float32)),
         in_specs=[pl.BlockSpec(memory_space=pltpu.HBM), pl.BlockSpec(memory_space=pl.ANY)],
-        out_specs=pl.BlockSpec(memory_space=pltpu.VMEM),
+        out_specs=(pl.BlockSpec(memory_space=pltpu.VMEM),) * 3,
         scratch_shapes=[
             pltpu.SMEM((species,), jnp.float32),
             pltpu.VMEM(block, jnp.float32),
             pltpu.VMEM(block, jnp.float32),
-            pltpu.VMEM((2, species, REACH, cy, cz), jnp.float32),
+            pltpu.VMEM((layers, cy, cz), jnp.float32),
+            pltpu.VMEM((species, 2, REACH, cy, cz), jnp.float32),
             pltpu.VMEM((sides,) + block, jnp.float32),
             pltpu.VMEM((2, rows_packed, cx, cy, cz), jnp.float32),
             pltpu.VMEM((2, rows_packed, cx, cy, cz), jnp.float32),
-            dma((2,)),
             dma,
             dma,
-            dma((sides, 2)),
+            dma((2,)),
+            dma((sides,)),
             dma((sides, pieces)),
-            dma,
             dma,
             pltpu.SemaphoreType.REGULAR((3,)),
             pltpu.SemaphoreType.REGULAR,
@@ -322,6 +452,29 @@
         compiler_params=pltpu.CompilerParams(collective_id=0, has_side_effects=True, vmem_limit_bytes=56 * 1024 * 1024),
         name="filter_pass",
     )(fields, strength)
+    if early == pieces:
+        return filtered
+    vmem, hbm = pl.BlockSpec(memory_space=pltpu.VMEM), pl.BlockSpec(memory_space=pltpu.HBM)
+    small = 4 * 1024 * 1024
+    written, token = pl.pallas_call(
+        functools.partial(write_kernel, late),
+        out_shape=(pltpu.HBM(block, jnp.float32), pltpu.VMEM((8, 128), jnp.float32)),
+        in_specs=[vmem], out_specs=(hbm, vmem), scratch_shapes=[dma],
+        compiler_params=pltpu.CompilerParams(vmem_limit_bytes=small), name="write",
+    )(filtered)
+    late_out = pl.pallas_call(
+        functools.partial(late_kernel, ny, cuts[-LATE:]),
+        out_shape=pltpu.VMEM((late,) + block[1:], jnp.float32),
+        in_specs=[vmem] * 4, out_specs=vmem,
+        scratch_shapes=[pltpu.VMEM((sides, late) + block[1:], jnp.float32), dma((sides,)), dma((sides, LATE))],
+        compiler_params=pltpu.CompilerParams(collective_id=1, has_side_effects=True, vmem_limit_bytes=small), name="late",
+    )(filtered, late_u, late_gain, token)
+    return pl.pallas_call(
+        close_kernel,
+        out_shape=pltpu.HBM(block, jnp.float32),
+        in_specs=[hbm, vmem], out_specs=hbm, scratch_shapes=[dma], input_output_aliases={0: 0},
+        compiler_params=pltpu.CompilerParams(vmem_limit_bytes=small), name="close",
+    )(written, late_out)
 
 
 def solution(mesh):

time: 27 us -> 26.7 us (0.989)
  local copies, waits for them, and re-layouts: 0.97 us -> 0 us
  Pallas kernels: 25.9 us -> 26.5 us
    unnamed x1 -> x0, local copies, waits for them, and re-layouts: 0.97 us -> none
    pallas_call x1 -> x4, Pallas kernels: 25.9 us -> 26.5 us  [the longest x1 20.3 us: local(): pl.pallas_call(functools.partial(kernel, nx, ny, nz, cuts, early, late),...]
where the time goes in v8:
time: 26.7 us; the launch traced here: 26.5 us
  Pallas kernels  26.5 us (99%)
    pallas_call x1, Pallas kernels, local(): pl.pallas_call(functools.partial(kernel, nx, ny, nz, cuts, early, late),...  20.3 us
    pallas_call x1, Pallas kernels, local(): pl.pallas_call(functools.partial(late_kernel, ny, cuts[-LATE:]), out_shap...  4.63 us
    pallas_call x1, Pallas kernels, local(): pl.pallas_call(functools.partial(write_kernel, late), out_shape=(pltpu.HB...  0.92 us
    pallas_call x1, Pallas kernels, local(): pl.pallas_call(close_kernel, out_shape=pltpu.HBM(block, jnp.float32), in_...  0.7 us

profile of v8, /device:TPU:1, one launch (start us, length us, event | category | flops | bytes accessed | tf_op | source)
XLA Modules:
  0.0 26.5 jit_solution(6648766565946638607)
XLA Ops:
  0.0 20.3 %filter_pass.1 = (f32[32,8,8,128]{3,2,1,0:T(8,128)S(1)}, f32[6,8,8,128]{3,2,1,0:T(8,128)S(1)}, f32[6,8,128]{2,1,0:T(8,128)S(1)}) custom-call(f32[32,8,8,128]{3,2,1,0:T(8,128)} %fields.1, f32[32]{0:T(128)} %strength_in.1), custom_call_target="tpu_custom_call" | custom-call | tf_op jit(solution)/shard_map/filter_pass/pallas_call | solution.py:428
  20.3 0.9 %write.1 = (f32[32,8,8,128]{3,2,1,0:T(8,128)}, f32[8,128]{1,0:T(8,128)S(1)}) custom-call(f32[32,8,8,128]{3,2,1,0:T(8,128)S(1)} %get-tuple-element.10.filtered), custom_call_target="tpu_custom_call" | custom-call | tf_op jit(solution)/shard_map/write/pallas_call | solution.py:459
  21.2 4.6 %late.1.late_out = f32[6,8,8,128]{3,2,1,0:T(8,128)S(1)} custom-call(f32[32,8,8,128]{3,2,1,0:T(8,128)S(1)} %get-tuple-element.10.filtered, f32[6,8,8,128]{3,2,1,0:T(8,128)S(1)} %get-tuple-element.12.late_u, f32[6,8,128]{2,1,0:T(8,128)S(1)} %get-tuple-element.13.late_gain, f32[8,128]{1,0:T(8,128)S(1)} %get-tuple-element.14._), custom_call_target="tpu_custom_call" | custom-call | tf_op jit(solution)/shard_map/late/pallas_call | solution.py:465
  25.8 0.7 %close.1 = f32[32,8,8,128]{3,2,1,0:T(8,128)} custom-call(f32[32,8,8,128]{3,2,1,0:T(8,128)} %get-tuple-element.11._, f32[6,8,8,128]{3,2,1,0:T(8,128)S(1)} %late.1.late_out), custom_call_target="tpu_custom_call", output_to_operand_aliasing={{}: (0, {})} | custom-call | tf_op jit(solution)/shard_map/close/pallas_call | solution.py:472

commit v9 on v7

--- a/solution.py
+++ b/solution.py
@@ -119,15 +119,18 @@
 
     held = early < len(cuts)
     mark = sum(cuts[:early])
-    y_copies = []
-    for k, (begin, size) in enumerate(spans):
-        part = pl.ds(begin, size)
-        y_copies.append([
+
+    def y_row(k, source):
+        part = pl.ds(*spans[k])
+        return [
             pltpu.make_async_remote_copy(
-                src_ref=(fields if k < early else u).at[part], dst_ref=ys.at[side, part],
+                src_ref=source.at[part], dst_ref=ys.at[side, part],
                 send_sem=y_send.at[side] if k < early else sent, recv_sem=y_recv.at[side, k],
                 device_id=(px, peer, pz), device_id_type=MESH)
-            for side, peer in enumerate(y_peers)])
+            for side, peer in enumerate(y_peers)]
+
+    y_copies = [y_row(k, fields if k < early else u) for k in range(len(spans))]
+    loaded_copies = [y_row(k, u) for k in range(early)]
     x_copies = [
         pltpu.make_async_remote_copy(
             src_ref=u.at[:, pl.ds(begin, REACH)], dst_ref=xs.at[side],
@@ -173,13 +176,18 @@
 
     greeters = (pz > 0).astype(jnp.int32) + (2 * (1 - lax.rem(px, 2)) if paired else 2)
     pl.semaphore_wait(barrier, len(y_peers) + greeters)
-    if relayed:
-        start_y(y_copies[:early - 1])
-        pl.when(source)(direct.start)
-        pl.when(jnp.logical_not(source))(lambda: start_y(y_copies[early - 1:early]))
-    else:
-        start_y(y_copies[:early])
+    def start_early():
+        if relayed:
+            start_y(y_copies[:early - 1])
+            pl.when(source)(direct.start)
+            pl.when(jnp.logical_not(source))(lambda: start_y(y_copies[early - 1:early]))
+        else:
+            start_y(y_copies[:early])
+
+    unloaded = lax.rem(py, 2) == 1
+    pl.when(unloaded)(start_early)
     load.wait()
+    pl.when(jnp.logical_not(unloaded))(lambda: start_y(loaded_copies))
     gains.start()
     if held:
         at_once = jnp.logical_not(jnp.logical_or(odd, relay_out) if relayed else odd)
@@ -335,6 +343,12 @@
         pl.when(jnp.logical_not(relay))(lambda: settle(tiles.at[pl.ds(0, layers)], sent))
     else:
         settle(tiles.at[pl.ds(0, layers)], sent)
+
+
+def write(filtered, out, done):
+    for s in range(filtered.shape[0]):
+        pltpu.make_async_copy(filtered.at[s], out.at[s], done).start()
+    pltpu.make_async_copy(filtered, out, done).wait()
 
 
 def local(nx, ny, nz, fields, strength):
@@ -348,7 +362,7 @@
     block = (species, cx, cy, cz)
     layers = 2 * species * REACH + 2 * rows_packed * cx + sides * species * cx + species * DETOUR
     dma = pltpu.SemaphoreType.DMA
-    return pl.pallas_call(
+    filtered = pl.pallas_call(
         functools.partial(kernel, nx, ny, nz, cuts, early),
         out_shape=pltpu.VMEM(block, jnp.float32),
         in_specs=[pl.BlockSpec(memory_space=pltpu.HBM), pl.BlockSpec(memory_space=pl.ANY)],
@@ -376,6 +390,15 @@
         compiler_params=pltpu.CompilerParams(collective_id=0, has_side_effects=True, vmem_limit_bytes=56 * 1024 * 1024),
         name="filter_pass",
     )(fields, strength)
+    return pl.pallas_call(
+        write,
+        out_shape=pltpu.HBM(block, jnp.float32),
+        in_specs=[pl.BlockSpec(memory_space=pltpu.VMEM)],
+        out_specs=pl.BlockSpec(memory_space=pltpu.HBM),
+        scratch_shapes=[dma],
+        compiler_params=pltpu.CompilerParams(vmem_limit_bytes=4 * 1024 * 1024),
+        name="write",
+    )(filtered)
 
 
 def solution(mesh):

time: 26.6 us -> 26.6 us (level)
  Pallas kernels: 25.4 us -> 26.4 us
  local copies, waits for them, and re-layouts: 0.97 us -> 0 us
    unnamed x1 -> x0, local copies, waits for them, and re-layouts: 0.97 us -> none
    pallas_call x0 -> x1, Pallas kernels: none -> 0.95 us  [local(): pl.pallas_call(write, out_shape=pltpu.HBM(block, jnp.float32), in_specs=[...]
where the time goes in v9:
time: 26.6 us; the launch traced here: 26.4 us
  Pallas kernels  26.4 us (99%)
    pallas_call x1, Pallas kernels, local(): pl.pallas_call(functools.partial(kernel, nx, ny, nz, cuts, early), out_sh...  25.4 us
    pallas_call x1, Pallas kernels, local(): pl.pallas_call(write, out_shape=pltpu.HBM(block, jnp.float32), in_specs=[...  0.95 us

profile of v9, /device:TPU:1, one launch (start us, length us, event | category | flops | bytes accessed | tf_op | source)
XLA Modules:
  0.0 26.4 jit_solution(12161560027067533539)
XLA Ops:
  0.0 25.4 %filter_pass.1.filtered = f32[32,8,8,128]{3,2,1,0:T(8,128)S(1)} custom-call(f32[32,8,8,128]{3,2,1,0:T(8,128)} %fields.1, f32[32]{0:T(128)} %strength_in.1), custom_call_target="tpu_custom_call" | custom-call | tf_op jit(solution)/shard_map/filter_pass/pallas_call | solution.py:365
  25.5 1.0 %write.1 = f32[32,8,8,128]{3,2,1,0:T(8,128)} custom-call(f32[32,8,8,128]{3,2,1,0:T(8,128)S(1)} %filter_pass.1.filtered), custom_call_target="tpu_custom_call" | custom-call | tf_op jit(solution)/shard_map/write/pallas_call | solution.py:393

commit v10 on v9

--- a/solution.py
+++ b/solution.py
@@ -10,7 +10,7 @@
 REACH = 5
 SLOT = 8
 WEIGHTS = [-252.0, 210.0, -120.0, 45.0, -10.0, 1.0]
-CUTS = (19, 5, 7, 1)
+CUTS = (19, 5, 6, 2)
 EARLY = 2
 DETOUR = 1
 AT_ONCE = (8, 4, 8)

time: 26.6 us -> 26.6 us (level)
  no operation moved by 1% of the time
where the time goes in v10:
time: 26.6 us; the launch traced here: 26.4 us
  Pallas kernels  26.4 us (99%)
    pallas_call x1, Pallas kernels, local(): pl.pallas_call(functools.partial(kernel, nx, ny, nz, cuts, early), out_sh...  25.5 us
    pallas_call x1, Pallas kernels, local(): pl.pallas_call(write, out_shape=pltpu.HBM(block, jnp.float32), in_specs=[...  0.95 us

profile of v10, /device:TPU:1, one launch (start us, length us, event | category | flops | bytes accessed | tf_op | source)
XLA Modules:
  0.0 26.4 jit_solution(4182467817341559868)
XLA Ops:
  0.0 25.5 %filter_pass.1.filtered = f32[32,8,8,128]{3,2,1,0:T(8,128)S(1)} custom-call(f32[32,8,8,128]{3,2,1,0:T(8,128)} %fields.1, f32[32]{0:T(128)} %strength_in.1), custom_call_target="tpu_custom_call" | custom-call | tf_op jit(solution)/shard_map/filter_pass/pallas_call | solution.py:365
  25.5 1.0 %write.1 = f32[32,8,8,128]{3,2,1,0:T(8,128)} custom-call(f32[32,8,8,128]{3,2,1,0:T(8,128)S(1)} %filter_pass.1.filtered), custom_call_target="tpu_custom_call" | custom-call | tf_op jit(solution)/shard_map/write/pallas_call | solution.py:393

commit v11 on v9

--- a/solution.py
+++ b/solution.py
@@ -115,7 +115,8 @@
         begin += size
     load = pltpu.make_async_copy(fields, u, in_sem)
     gains = pltpu.make_async_copy(strength_in, strength, in_sem)
-    load.start()
+    unloaded = lax.rem(py, 2) == 1
+    pl.when(jnp.logical_not(unloaded))(load.start)
 
     held = early < len(cuts)
     mark = sum(cuts[:early])
@@ -184,8 +185,8 @@
         else:
             start_y(y_copies[:early])
 
-    unloaded = lax.rem(py, 2) == 1
     pl.when(unloaded)(start_early)
+    pl.when(unloaded)(load.start)
     load.wait()
     pl.when(jnp.logical_not(unloaded))(lambda: start_y(loaded_copies))
     gains.start()

time: 26.6 us -> 26.6 us (level)
  no operation moved by 1% of the time
where the time goes in v11:
time: 26.6 us; the launch traced here: 26.4 us
  Pallas kernels  26.4 us (99%)
    pallas_call x1, Pallas kernels, local(): pl.pallas_call(functools.partial(kernel, nx, ny, nz, cuts, early), out_sh...  25.4 us
    pallas_call x1, Pallas kernels, local(): pl.pallas_call(write, out_shape=pltpu.HBM(block, jnp.float32), in_specs=[...  0.95 us

profile of v11, /device:TPU:1, one launch (start us, length us, event | category | flops | bytes accessed | tf_op | source)
XLA Modules:
  0.0 26.4 jit_solution(4779942737798178122)
XLA Ops:
  0.0 25.4 %filter_pass.1.filtered = f32[32,8,8,128]{3,2,1,0:T(8,128)S(1)} custom-call(f32[32,8,8,128]{3,2,1,0:T(8,128)} %fields.1, f32[32]{0:T(128)} %strength_in.1), custom_call_target="tpu_custom_call" | custom-call | tf_op jit(solution)/shard_map/filter_pass/pallas_call | solution.py:366
  25.4 1.0 %write.1 = f32[32,8,8,128]{3,2,1,0:T(8,128)} custom-call(f32[32,8,8,128]{3,2,1,0:T(8,128)S(1)} %filter_pass.1.filtered), custom_call_target="tpu_custom_call" | custom-call | tf_op jit(solution)/shard_map/write/pallas_call | solution.py:394

commit v12 on v11

--- a/solution.py
+++ b/solution.py
@@ -10,7 +10,7 @@
 REACH = 5
 SLOT = 8
 WEIGHTS = [-252.0, 210.0, -120.0, 45.0, -10.0, 1.0]
-CUTS = (19, 5, 7, 1)
+CUTS = (18, 6, 7, 1)
 EARLY = 2
 DETOUR = 1
 AT_ONCE = (8, 4, 8)

time: 26.6 us -> 26.6 us (level)
  no operation moved by 1% of the time
where the time goes in v12:
time: 26.6 us; the launch traced here: 26.4 us
  Pallas kernels  26.4 us (99%)
    pallas_call x1, Pallas kernels, local(): pl.pallas_call(functools.partial(kernel, nx, ny, nz, cuts, early), out_sh...  25.4 us
    pallas_call x1, Pallas kernels, local(): pl.pallas_call(write, out_shape=pltpu.HBM(block, jnp.float32), in_specs=[...  0.95 us

profile of v12, /device:TPU:1, one launch (start us, length us, event | category | flops | bytes accessed | tf_op | source)
XLA Modules:
  0.0 26.4 jit_solution(1118727834781151012)
XLA Ops:
  0.0 25.4 %filter_pass.1.filtered = f32[32,8,8,128]{3,2,1,0:T(8,128)S(1)} custom-call(f32[32,8,8,128]{3,2,1,0:T(8,128)} %fields.1, f32[32]{0:T(128)} %strength_in.1), custom_call_target="tpu_custom_call" | custom-call | tf_op jit(solution)/shard_map/filter_pass/pallas_call | solution.py:366
  25.4 1.0 %write.1 = f32[32,8,8,128]{3,2,1,0:T(8,128)} custom-call(f32[32,8,8,128]{3,2,1,0:T(8,128)S(1)} %filter_pass.1.filtered), custom_call_target="tpu_custom_call" | custom-call | tf_op jit(solution)/shard_map/write/pallas_call | solution.py:394
